TPU v7x, 32 devices: a whole 2x2x4 slice. The times are simulated.
32 devices in a mesh: videos: 2 (over x), tokens: 4 (over z), frames: 4 (over y, core).
Axes of the slice: x: 2, y: 2, z: 4, core: 2. Of those that a mesh axis runs over, the one named last changes fastest.
Arguments:
- z_queue: float32 [128, 256, 4], P(('videos', 'frames'), 'tokens'), parts along dimension 0
- ada_mod: float32 [128, 3, 6, 1024], P(('videos', 'frames')), parts along dimension 0
- step_size: float32 [128], P(('videos', 'frames')), parts along dimension 0
- new_noise: float32 [4, 256, 4], P('videos', 'tokens'), parts along dimension 0
- lag_bias: float32 [3, 16, 16], replicated
- w_in: bfloat16 [4, 1024], replicated
- w_out: bfloat16 [1024, 4], replicated
- w_sqkv: bfloat16 [3, 1024, 3, 16, 64], replicated
- w_so: bfloat16 [3, 16, 64, 1024], replicated
- w_tqkv: bfloat16 [3, 1024, 3, 16, 64], replicated
- w_to: bfloat16 [3, 16, 64, 1024], replicated
- w_up: bfloat16 [3, 1024, 4096], replicated
- w_down: bfloat16 [3, 4096, 1024], replicated
Outputs:
- output 1: float32 [4, 256, 4], P('videos', ('tokens', 'frames')), parts along dimension 0
- output 2: float32 [128, 256, 4], P(('videos', 'frames'), 'tokens'), parts along dimension 0
There are 2 independent parts. A program takes and returns all parts, laid end to end along the dimension named above; an argument that names none is the same for every part.
All inputs are finite; a program needn't handle non-finite values.
Results may differ from a plain program's by a relative error of at most 0.00847983.
Values are sent between devices in bfloat16 or wider.
A program may use at most 1 GiB of HBM per device.

v0:
```python
import jax
import jax.numpy as jnp
from jax import lax
from jax.sharding import PartitionSpec as P


def layer_norm(xres):
    row_mean = jnp.mean(xres, axis=-1, keepdims=True)
    centered = xres - row_mean
    row_var = jnp.mean(centered * centered, axis=-1, keepdims=True)
    return centered * lax.rsqrt(row_var + 1e-6)


def modulate(xres, mod_l, which):
    shift_vec = mod_l[..., None, 2 * which, :]
    scale_vec = mod_l[..., None, 2 * which + 1, :]
    return (layer_norm(xres) * (1.0 + scale_vec) + shift_vec).astype(jnp.bfloat16)


def spatial_block(u_act, w_qkv, w_proj):
    qkv_loc = jnp.einsum('apd,dthe->apthe', u_act, w_qkv, preferred_element_type=jnp.float32).astype(jnp.bfloat16)
    qkv_full = lax.all_to_all(qkv_loc, 'tokens', 3, 1, tiled=True)
    head_dim = qkv_full.shape[-1]
    scores = jnp.einsum('aqhe,akhe->ahqk', qkv_full[:, :, 0], qkv_full[:, :, 1], preferred_element_type=jnp.float32) * head_dim ** -0.5
    attn_prob = jax.nn.softmax(scores, axis=-1).astype(jnp.bfloat16)
    attn_out = jnp.einsum('ahqk,akhe->aqhe', attn_prob, qkv_full[:, :, 2], preferred_element_type=jnp.float32).astype(jnp.bfloat16)
    attn_loc = lax.all_to_all(attn_out, 'tokens', 1, 2, tiled=True)
    return jnp.einsum('aphe,hed->apd', attn_loc, w_proj, preferred_element_type=jnp.float32)


def temporal_qkv(u_act, w_qkv):
    return jnp.einsum('apd,dthe->apthe', u_act, w_qkv, preferred_element_type=jnp.float32).astype(jnp.bfloat16)


def temporal_attend(qkv_loc, halo_kv, lag_bias, w_proj, has_prev):
    n_frames = qkv_loc.shape[0]
    window = lag_bias.shape[-1]
    head_dim = qkv_loc.shape[-1]
    keys_ext = jnp.concatenate([halo_kv[:, :, 0], qkv_loc[:, :, 1]], axis=0)
    vals_ext = jnp.concatenate([halo_kv[:, :, 1], qkv_loc[:, :, 2]], axis=0)
    scores = jnp.einsum('aphe,bphe->phab', qkv_loc[:, :, 0], keys_ext, preferred_element_type=jnp.float32) * head_dim ** -0.5
    query_idx = jnp.arange(n_frames)[:, None]
    key_idx = jnp.arange(n_frames + window - 1)[None, :]
    lag_mat = query_idx + window - 1 - key_idx
    valid = (lag_mat >= 0) & (lag_mat < window) & ((key_idx >= window - 1) | has_prev)
    bias_mat = jnp.take(lag_bias, jnp.clip(lag_mat, 0, window - 1), axis=1)
    scores = jnp.where(valid, scores + bias_mat, -1e30)
    attn_prob = jax.nn.softmax(scores, axis=-1).astype(jnp.bfloat16)
    attn_out = jnp.einsum('phab,bphe->aphe', attn_prob, vals_ext, preferred_element_type=jnp.float32).astype(jnp.bfloat16)
    return jnp.einsum('aphe,hed->apd', attn_out, w_proj, preferred_element_type=jnp.float32)


def mlp_block(u_act, w_up, w_down):
    hidden = jnp.einsum('apd,dk->apk', u_act, w_up, preferred_element_type=jnp.float32)
    return jnp.einsum('apk,kd->apd', jax.nn.gelu(hidden, approximate=True).astype(jnp.bfloat16), w_down, preferred_element_type=jnp.float32)


def solution(mesh):
    n_blocks = mesh.shape['frames']
    to_next = [(i, i + 1) for i in range(n_blocks - 1)]
    to_prev = [(i + 1, i) for i in range(n_blocks - 1)]
    slot_spec = P(('videos', 'frames'), 'tokens', None)
    mod_spec = P(('videos', 'frames'), None, None, None)
    step_spec = P(('videos', 'frames'))
    noise_spec = P('videos', 'tokens', None)
    emit_spec = P('videos', ('tokens', 'frames'), None)

    def body(z_loc, mod_loc, step_loc, noise_loc, lag_bias, w_in, w_out, w_sqkv, w_so, w_tqkv, w_to, w_up, w_down):
        frame_pos = lax.axis_index('frames')
        has_prev = frame_pos > 0
        n_layers = w_sqkv.shape[0]
        window = lag_bias.shape[-1]
        n_frames = z_loc.shape[0]
        step_col = step_loc[:, None, None]

        def one_step(z_cur, noise_frame):
            xres = jnp.einsum('apc,cd->apd', z_cur.astype(jnp.bfloat16), w_in, preferred_element_type=jnp.float32).astype(jnp.bfloat16).astype(jnp.float32)
            for layer in range(n_layers):
                mod_l = mod_loc[:, layer]
                xres = xres + spatial_block(modulate(xres, mod_l, 0), w_sqkv[layer], w_so[layer])
                qkv_loc = temporal_qkv(modulate(xres, mod_l, 1), w_tqkv[layer])
                halo_kv = lax.ppermute(qkv_loc[n_frames - window + 1:, :, 1:], 'frames', to_next)
                xres = xres + temporal_attend(qkv_loc, halo_kv, lag_bias[layer], w_to[layer], has_prev)
                xres = xres + mlp_block(modulate(xres, mod_l, 2), w_up[layer], w_down[layer])
            velocity = jnp.einsum('apd,dc->apc', layer_norm(xres).astype(jnp.bfloat16), w_out, preferred_element_type=jnp.float32)
            z_new = z_cur + step_col * velocity
            incoming = lax.ppermute(z_new[0], 'frames', to_prev)
            incoming = jnp.where(frame_pos == n_blocks - 1, noise_frame, incoming)
            emit_loc = lax.psum_scatter(jnp.where(frame_pos == 0, z_new[0], 0.0), 'frames', scatter_dimension=0, tiled=True)
            return jnp.concatenate([z_new[1:], incoming[None]], axis=0), emit_loc

        z_out, emitted = lax.scan(one_step, z_loc, noise_loc)
        return emitted, z_out

    return jax.shard_map(body, mesh=mesh, in_specs=(slot_spec, mod_spec, step_spec, noise_spec) + (P(),) * 9, out_specs=(emit_spec, slot_spec), check_vma=False)
```

profile of v0, /device:TPU:0, one launch (start us, length us, event | category | flops | bytes accessed | tf_op | source)
XLA Modules:
  0.0 3325.1 jit_solution(1365301702069538767)
XLA Ops:
  8.7 3308.6 %while.16 = (s32[]{:T(128)}, f32[16,64,4]{1,2,0:T(4,128)S(1)}, f32[2,16,4]{1,2,0:T(4,128)}, f32[16,1,1]{0,2,1:T(1,128)}, bf16[4,1024]{1,0:T(4,128)(2,1)}, /*inde...) while((s32[]{:T(128)}, f32[16,64,4]{1,2,0:T(4,128)S(1)}, ...), condition=%wide.region_34.36_spmd, body=%wide.region_0.35_spmd.sunk | while | flops 107055775744 | bytes 1338708608 | solution.py:92
  48.3 146.0 %all_to_all.246 = bf16[4,2,393216]{2,1,0:T(2,128)(2,1)} all-to-all(bf16[4,2,393216]{2,1,0:T(2,128)(2,1)} %reshape.294), channel_id=1, replica_groups=mesh['videos'=2,'tokens'=4,'frames'=4] {'tokens'}, dimensions={0} | all-to-all | bytes 12582912 | tf_op jit(solution)/shard_map/while/body/eval_jaxpr/all_to_all | solution.py:22
  293.2 52.3 %all_to_all.247 = bf16[4,2,131072]{2,1,0:T(2,128)(2,1)} all-to-all(bf16[4,2,131072]{2,1,0:T(2,128)(2,1)S(1)} %reshape.296), channel_id=1, replica_groups=mesh['videos'=2,'tokens'=4,'frames'=4] {'tokens'}, dimensions={0} | all-to-all | bytes 4194304 | tf_op jit(solution)/shard_map/while/body/eval_jaxpr/all_to_all | solution.py:27
  421.1 32.1 fusion.414
  567.1 78.8 %all_to_all.248 = bf16[4,2,393216]{2,1,0:T(2,128)(2,1)} all-to-all(bf16[4,2,393216]{2,1,0:T(2,128)(2,1)} %reshape.302), channel_id=1, replica_groups=mesh['videos'=2,'tokens'=4,'frames'=4] {'tokens'}, dimensions={0} | all-to-all | bytes 12582912 | tf_op jit(solution)/shard_map/while/body/eval_jaxpr/all_to_all | solution.py:22
  744.8 32.4 all_to_all.249
  824.3 77.0 %collective-permute-start.1 = (bf16[15,64,2,16,64]{4,1,3,0,2:T(8,128)(2,1)}, bf16[15,64,2,16,64]{4,1,3,0,2:T(8,128)(2,1)S(1)}, u32[]{:S(2)}, u32[]{:S(2)}) collective-permute-start(bf16[15,64,2,16,64]{4,1,3,0,2:T(8,128)(2,1)} %copy.217), channel_id=1, source_target_pairs={{0,1},{1,2},{2,3},{4,5},{5,6},{6,7},{8,9},{9,10},{10,11},{12,13},{... | collective-permute-start | bytes 11796488 | tf_op jit(solution)/shard_map/while/body/eval_jaxpr/ppermute | solution.py:82
  934.2 33.5 %fusion.423 = f32[64,16,16,31]{3,2,1,0:T(8,128)} fusion(bf16[31,64,16,64]{3,1,2,0:T(8,128)(2,1)} %pad_maximum_fusion.14, bf16[16,64,16,64]{3,1,2,0:T(8,128)(2,1)} %get-tuple-element.756), kind=kOutput, calls=%fused_computation.66.clone.1 | convolution fusion | flops 65011712 | bytes 8192000 | tf_op jit(solution)/shard_map/while/body/eval_jaxpr/aphe,bphe->phab/dot_general | solution.py:41
  1081.4 78.8 %all_to_all.250 = bf16[4,2,393216]{2,1,0:T(2,128)(2,1)} all-to-all(bf16[4,2,393216]{2,1,0:T(2,128)(2,1)} %reshape.306), channel_id=1, replica_groups=mesh['videos'=2,'tokens'=4,'frames'=4] {'tokens'}, dimensions={0} | all-to-all | bytes 12582912 | tf_op jit(solution)/shard_map/while/body/eval_jaxpr/all_to_all | solution.py:22
  1259.0 32.7 all_to_all.251
  1338.7 80.2 %collective-permute-start.2 = (bf16[15,64,2,16,64]{4,1,3,0,2:T(8,128)(2,1)}, bf16[15,64,2,16,64]{4,1,3,0,2:T(8,128)(2,1)}, u32[]{:S(2)}, u32[]{:S(2)}) collective-permute-start(bf16[15,64,2,16,64]{4,1,3,0,2:T(8,128)(2,1)} %copy.222), channel_id=1, source_target_pairs={{0,1},{1,2},{2,3},{4,5},{5,6},{6,7},{8,9},{9,10},{10,11},{12,13},{... | collective-permute-start | bytes 11796488 | tf_op jit(solution)/shard_map/while/body/eval_jaxpr/ppermute | solution.py:82
  1451.2 33.6 %fusion.430 = f32[64,16,16,31]{3,2,1,0:T(8,128)} fusion(bf16[31,64,16,64]{3,1,2,0:T(8,128)(2,1)} %pad_maximum_fusion.16, bf16[16,64,16,64]{3,1,2,0:T(8,128)(2,1)} %get-tuple-element.778), kind=kOutput, calls=%fused_computation.62.clone.1 | convolution fusion | flops 65011712 | bytes 8192000 | tf_op jit(solution)/shard_map/while/body/eval_jaxpr/aphe,bphe->phab/dot_general | solution.py:41
  1567.5 78.1 %collective-permute-done.3 = f32[64,4]{0,1:T(4,128)S(1)} collective-permute-done((f32[64,4]{0,1:T(4,128)S(1)}, f32[64,4]{0,1:T(4,128)S(1)}, u32[]{:S(2)}, u32[]{:S(2)}) %collective-permute-start.3) | collective-permute-done | bytes 1056 | tf_op jit(solution)/shard_map/while/body/eval_jaxpr/ppermute | solution.py:87
  1706.8 144.3 %all_to_all.246 = bf16[4,2,393216]{2,1,0:T(2,128)(2,1)} all-to-all(bf16[4,2,393216]{2,1,0:T(2,128)(2,1)} %reshape.294), channel_id=1, replica_groups=mesh['videos'=2,'tokens'=4,'frames'=4] {'tokens'}, dimensions={0} | all-to-all | bytes 12582912 | tf_op jit(solution)/shard_map/while/body/eval_jaxpr/all_to_all | solution.py:22
  1950.1 51.3 %all_to_all.247 = bf16[4,2,131072]{2,1,0:T(2,128)(2,1)} all-to-all(bf16[4,2,131072]{2,1,0:T(2,128)(2,1)S(1)} %reshape.296), channel_id=1, replica_groups=mesh['videos'=2,'tokens'=4,'frames'=4] {'tokens'}, dimensions={0} | all-to-all | bytes 4194304 | tf_op jit(solution)/shard_map/while/body/eval_jaxpr/all_to_all | solution.py:27
  2223.0 78.8 %all_to_all.248 = bf16[4,2,393216]{2,1,0:T(2,128)(2,1)} all-to-all(bf16[4,2,393216]{2,1,0:T(2,128)(2,1)} %reshape.302), channel_id=1, replica_groups=mesh['videos'=2,'tokens'=4,'frames'=4] {'tokens'}, dimensions={0} | all-to-all | bytes 12582912 | tf_op jit(solution)/shard_map/while/body/eval_jaxpr/all_to_all | solution.py:22
  2400.7 39.6 %all_to_all.249 = bf16[4,2,131072]{2,1,0:T(2,128)(2,1)} all-to-all(bf16[4,2,131072]{2,1,0:T(2,128)(2,1)S(1)} %reshape.304), channel_id=1, replica_groups=mesh['videos'=2,'tokens'=4,'frames'=4] {'tokens'}, dimensions={0} | all-to-all | bytes 4194304 | tf_op jit(solution)/shard_map/while/body/eval_jaxpr/all_to_all | solution.py:27
  2487.3 63.6 %collective-permute-start.1 = (bf16[15,64,2,16,64]{4,1,3,0,2:T(8,128)(2,1)}, bf16[15,64,2,16,64]{4,1,3,0,2:T(8,128)(2,1)S(1)}, u32[]{:S(2)}, u32[]{:S(2)}) collective-permute-start(bf16[15,64,2,16,64]{4,1,3,0,2:T(8,128)(2,1)} %copy.217), channel_id=1, source_target_pairs={{0,1},{1,2},{2,3},{4,5},{5,6},{6,7},{8,9},{9,10},{10,11},{12,13},{... | collective-permute-start | bytes 11796488 | tf_op jit(solution)/shard_map/while/body/eval_jaxpr/ppermute | solution.py:82
  2583.8 33.5 %fusion.423 = f32[64,16,16,31]{3,2,1,0:T(8,128)} fusion(bf16[31,64,16,64]{3,1,2,0:T(8,128)(2,1)} %pad_maximum_fusion.14, bf16[16,64,16,64]{3,1,2,0:T(8,128)(2,1)} %get-tuple-element.756), kind=kOutput, calls=%fused_computation.66.clone.1 | convolution fusion | flops 65011712 | bytes 8192000 | tf_op jit(solution)/shard_map/while/body/eval_jaxpr/aphe,bphe->phab/dot_general | solution.py:41
  2731.0 78.8 %all_to_all.250 = bf16[4,2,393216]{2,1,0:T(2,128)(2,1)} all-to-all(bf16[4,2,393216]{2,1,0:T(2,128)(2,1)} %reshape.306), channel_id=1, replica_groups=mesh['videos'=2,'tokens'=4,'frames'=4] {'tokens'}, dimensions={0} | all-to-all | bytes 12582912 | tf_op jit(solution)/shard_map/while/body/eval_jaxpr/all_to_all | solution.py:22
  2908.7 32.7 all_to_all.251
  2988.4 79.1 %collective-permute-start.2 = (bf16[15,64,2,16,64]{4,1,3,0,2:T(8,128)(2,1)}, bf16[15,64,2,16,64]{4,1,3,0,2:T(8,128)(2,1)}, u32[]{:S(2)}, u32[]{:S(2)}) collective-permute-start(bf16[15,64,2,16,64]{4,1,3,0,2:T(8,128)(2,1)} %copy.222), channel_id=1, source_target_pairs={{0,1},{1,2},{2,3},{4,5},{5,6},{6,7},{8,9},{9,10},{10,11},{12,13},{... | collective-permute-start | bytes 11796488 | tf_op jit(solution)/shard_map/while/body/eval_jaxpr/ppermute | solution.py:82
  3099.8 33.6 %fusion.430 = f32[64,16,16,31]{3,2,1,0:T(8,128)} fusion(bf16[31,64,16,64]{3,1,2,0:T(8,128)(2,1)} %pad_maximum_fusion.16, bf16[16,64,16,64]{3,1,2,0:T(8,128)(2,1)} %get-tuple-element.778), kind=kOutput, calls=%fused_computation.62.clone.1 | convolution fusion | flops 65011712 | bytes 8192000 | tf_op jit(solution)/shard_map/while/body/eval_jaxpr/aphe,bphe->phab/dot_general | solution.py:41
  3216.1 78.1 %collective-permute-done.3 = f32[64,4]{0,1:T(4,128)S(1)} collective-permute-done((f32[64,4]{0,1:T(4,128)S(1)}, f32[64,4]{0,1:T(4,128)S(1)}, u32[]{:S(2)}, u32[]{:S(2)}) %collective-permute-start.3) | collective-permute-done | bytes 1056 | tf_op jit(solution)/shard_map/while/body/eval_jaxpr/ppermute | solution.py:87
  (462 shorter events, 1838.3 us)
Async XLA Ops:
  9.1 388.3 %copy-start.29 = (f32[3,16,16]{1,2,0:T(8,128)}, f32[3,16,16]{1,2,0:T(8,128)S(1)}, u32[]{:S(2)}) copy-start(f32[3,16,16]{1,2,0:T(8,128)S(1)} %get-tuple-element.838) | copy-start | bytes 9220 | tf_op jit(solution)/shard_map/while
  9.2 1656.7 %reduce-scatter.6.cloned.1.call-start = ((), (), s32[]{:S(2)}) async-start(), calls=%async_computation.7 | async-start | bytes 40960 | tf_op jit(solution)/shard_map/while
  392.7 17.2 collective-permute-start
  401.8 51.4 %copy-start.32 = (pred[16,31]{1,0:T(8,128)(4,1)}, pred[16,31]{1,0:T(8,128)(4,1)S(1)}, u32[]{:S(2)}) copy-start(pred[16,31]{1,0:T(8,128)(4,1)S(1)} %get-tuple-element.734) | copy-start | bytes 1492 | tf_op jit(solution)/shard_map/while
  824.3 88.5 %collective-permute-start.1 = (bf16[15,64,2,16,64]{4,1,3,0,2:T(8,128)(2,1)}, bf16[15,64,2,16,64]{4,1,3,0,2:T(8,128)(2,1)S(1)}, u32[]{:S(2)}, u32[]{:S(2)}) collective-permute-start(bf16[15,64,2,16,64]{4,1,3,0,2:T(8,128)(2,1)} %copy.217), channel_id=1, source_target_pairs={{0,1},{1,2},{2,3},{4,5},{5,6},{6,7},{8,9},{9,10},{10,11},{12,13},{... | collective-permute-start | bytes 11796488 | tf_op jit(solution)/shard_map/while/body/eval_jaxpr/ppermute | solution.py:82
  934.2 46.7 %slice-start.2 = ((s8[8126464]{0:T(1024)(128)(4,1)}), s8[3932160]{0:T(1024)(128)(4,1)S(1)}, s32[]{:S(2)}) async-start(s8[8126464]{0:T(1024)(128)(4,1)} %bitcast.564), calls=%async_computation.10 | async-start | bytes 7864320 | tf_op jit(solution)/shard_map/while
  1338.7 89.2 %collective-permute-start.2 = (bf16[15,64,2,16,64]{4,1,3,0,2:T(8,128)(2,1)}, bf16[15,64,2,16,64]{4,1,3,0,2:T(8,128)(2,1)}, u32[]{:S(2)}, u32[]{:S(2)}) collective-permute-start(bf16[15,64,2,16,64]{4,1,3,0,2:T(8,128)(2,1)} %copy.222), channel_id=1, source_target_pairs={{0,1},{1,2},{2,3},{4,5},{5,6},{6,7},{8,9},{9,10},{10,11},{12,13},{... | collective-permute-start | bytes 11796488 | tf_op jit(solution)/shard_map/while/body/eval_jaxpr/ppermute | solution.py:82
  1451.2 46.8 %slice-start = ((s8[8126464]{0:T(1024)(128)(4,1)}), s8[3932160]{0:T(1024)(128)(4,1)S(1)}, s32[]{:S(2)}) async-start(s8[8126464]{0:T(1024)(128)(4,1)} %bitcast.562), calls=%async_computation.8 | async-start | bytes 7864320 | tf_op jit(solution)/shard_map/while
  1559.4 86.1 %copy-start.35 = (f32[2,64,4]{1,2,0:T(4,128)S(1)}, f32[2,64,4]{1,2,0:T(4,128)}, u32[]{:S(2)}) copy-start(f32[2,64,4]{1,2,0:T(4,128)} %get-tuple-element.844) | copy-start | bytes 6148 | tf_op jit(solution)/shard_map/while
  1559.4 107.2 %copy-start.37 = (f32[2,16,4]{1,2,0:T(4,128)S(1)}, f32[2,16,4]{1,2,0:T(4,128)}, u32[]{:S(2)}) copy-start(f32[2,16,4]{1,2,0:T(4,128)} %get-tuple-element.811) | copy-start | bytes 1540 | tf_op jit(solution)/shard_map/while
  1559.4 107.8 %copy-start.30 = (f32[3,16,16]{1,2,0:T(8,128)S(1)}, f32[3,16,16]{1,2,0:T(8,128)}, u32[]{:S(2)}) copy-start(f32[3,16,16]{1,2,0:T(8,128)} %copy-done.29) | copy-start | bytes 9220 | tf_op jit(solution)/shard_map/while
  1565.5 80.1 %collective-permute-start.3 = (f32[64,4]{0,1:T(4,128)S(1)}, f32[64,4]{0,1:T(4,128)S(1)}, u32[]{:S(2)}, u32[]{:S(2)}) collective-permute-start(f32[64,4]{0,1:T(4,128)S(1)} %slice_bitcast_fusion.90), channel_id=1, source_target_pairs={{1,0},{2,1},{3,2},{5,4},{6,5},{7,6},{9,8},{10,9},{11,10},{13,12},{... | collective-permute-start | bytes 3080 | tf_op jit(solution)/shard_map/while/body/eval_jaxpr/ppermute | solution.py:87
  1667.7 385.6 %copy-start.29 = (f32[3,16,16]{1,2,0:T(8,128)}, f32[3,16,16]{1,2,0:T(8,128)S(1)}, u32[]{:S(2)}) copy-start(f32[3,16,16]{1,2,0:T(8,128)S(1)} %get-tuple-element.838) | copy-start | bytes 9220 | tf_op jit(solution)/shard_map/while
  1667.7 1647.2 %reduce-scatter.6.cloned.1.call-start = ((), (), s32[]{:S(2)}) async-start(), calls=%async_computation.7 | async-start | bytes 40960 | tf_op jit(solution)/shard_map/while
  2048.6 17.2 collective-permute-start
  2057.7 51.4 %copy-start.32 = (pred[16,31]{1,0:T(8,128)(4,1)}, pred[16,31]{1,0:T(8,128)(4,1)S(1)}, u32[]{:S(2)}) copy-start(pred[16,31]{1,0:T(8,128)(4,1)S(1)} %get-tuple-element.734) | copy-start | bytes 1492 | tf_op jit(solution)/shard_map/while
  2487.3 75.1 %collective-permute-start.1 = (bf16[15,64,2,16,64]{4,1,3,0,2:T(8,128)(2,1)}, bf16[15,64,2,16,64]{4,1,3,0,2:T(8,128)(2,1)S(1)}, u32[]{:S(2)}, u32[]{:S(2)}) collective-permute-start(bf16[15,64,2,16,64]{4,1,3,0,2:T(8,128)(2,1)} %copy.217), channel_id=1, source_target_pairs={{0,1},{1,2},{2,3},{4,5},{5,6},{6,7},{8,9},{9,10},{10,11},{12,13},{... | collective-permute-start | bytes 11796488 | tf_op jit(solution)/shard_map/while/body/eval_jaxpr/ppermute | solution.py:82
  2583.8 46.7 %slice-start.2 = ((s8[8126464]{0:T(1024)(128)(4,1)}), s8[3932160]{0:T(1024)(128)(4,1)S(1)}, s32[]{:S(2)}) async-start(s8[8126464]{0:T(1024)(128)(4,1)} %bitcast.564), calls=%async_computation.10 | async-start | bytes 7864320 | tf_op jit(solution)/shard_map/while
  2988.4 88.1 %collective-permute-start.2 = (bf16[15,64,2,16,64]{4,1,3,0,2:T(8,128)(2,1)}, bf16[15,64,2,16,64]{4,1,3,0,2:T(8,128)(2,1)}, u32[]{:S(2)}, u32[]{:S(2)}) collective-permute-start(bf16[15,64,2,16,64]{4,1,3,0,2:T(8,128)(2,1)} %copy.222), channel_id=1, source_target_pairs={{0,1},{1,2},{2,3},{4,5},{5,6},{6,7},{8,9},{9,10},{10,11},{12,13},{... | collective-permute-start | bytes 11796488 | tf_op jit(solution)/shard_map/while/body/eval_jaxpr/ppermute | solution.py:82
  3099.8 46.8 %slice-start = ((s8[8126464]{0:T(1024)(128)(4,1)}), s8[3932160]{0:T(1024)(128)(4,1)S(1)}, s32[]{:S(2)}) async-start(s8[8126464]{0:T(1024)(128)(4,1)} %bitcast.562), calls=%async_computation.8 | async-start | bytes 7864320 | tf_op jit(solution)/shard_map/while
  3208.0 86.1 %copy-start.35 = (f32[2,64,4]{1,2,0:T(4,128)S(1)}, f32[2,64,4]{1,2,0:T(4,128)}, u32[]{:S(2)}) copy-start(f32[2,64,4]{1,2,0:T(4,128)} %get-tuple-element.844) | copy-start | bytes 6148 | tf_op jit(solution)/shard_map/while
  3208.0 107.6 %copy-start.37 = (f32[2,16,4]{1,2,0:T(4,128)S(1)}, f32[2,16,4]{1,2,0:T(4,128)}, u32[]{:S(2)}) copy-start(f32[2,16,4]{1,2,0:T(4,128)} %get-tuple-element.811) | copy-start | bytes 1540 | tf_op jit(solution)/shard_map/while
  3208.0 108.2 %copy-start.30 = (f32[3,16,16]{1,2,0:T(8,128)S(1)}, f32[3,16,16]{1,2,0:T(8,128)}, u32[]{:S(2)}) copy-start(f32[3,16,16]{1,2,0:T(8,128)} %copy-done.29) | copy-start | bytes 9220 | tf_op jit(solution)/shard_map/while
  3214.1 80.1 %collective-permute-start.3 = (f32[64,4]{0,1:T(4,128)S(1)}, f32[64,4]{0,1:T(4,128)S(1)}, u32[]{:S(2)}, u32[]{:S(2)}) collective-permute-start(f32[64,4]{0,1:T(4,128)S(1)} %slice_bitcast_fusion.90), channel_id=1, source_target_pairs={{1,0},{2,1},{3,2},{5,4},{6,5},{7,6},{9,8},{10,9},{11,10},{13,12},{... | collective-permute-start | bytes 3080 | tf_op jit(solution)/shard_map/while/body/eval_jaxpr/ppermute | solution.py:87
  (71 other events, 1047.7 us)
Sparse Core Ops, SparseCore 0:
  1567.7 98.1 reduce-scatter.5
  3216.2 98.5 reduce-scatter.5
where the time goes:
time: 3340 us; the launch traced here: 3330 us
  matrix products  900 us (27%)
  blocking collectives  846 us (25%)
  local copies, waits for them, and re-layouts  744 us (22%)
  starting transfers between devices  312 us (9%)
  other arithmetic  303 us (9%)
  waiting for transfers between devices  202 us (6%)
    all_to_all x6, blocking collectives, spatial_block(): qkv_full = lax.all_to_all(qkv_loc, 'tokens', 3, 1, tiled=True)  605 us
    ppermute x6, starting transfers between devices, one_step(): lax.ppermute(qkv_loc[n_frames - window + 1:, :, 1:], 'frames', to_next)  309 us
    while x202, local copies, waits for them, and re-layouts  273 us
    all_to_all x6, blocking collectives, spatial_block(): attn_loc = lax.all_to_all(attn_out, 'tokens', 1, 2, tiled=True)  241 us
    all_to_all x12, local copies, waits for them, and re-layouts, spatial_block(): qkv_full = lax.all_to_all(qkv_loc, 'tokens', 3, 1, tiled=True)  230 us
    dot_general x6, matrix products, temporal_attend(): jnp.einsum('aphe,bphe->phab', qkv_loc[:, :, 0], keys_ext, preferred_eleme...  198 us
    dot_general x6, matrix products, mlp_block(): jnp.einsum('apk,kd->apd', jax.nn.gelu(hidden, approximate=True).astype(jn...  161 us
    ppermute x2, waiting for transfers between devices, one_step(): incoming = lax.ppermute(z_new[0], 'frames', to_prev)  156 us
  transfers between devices with their start and end apart: 10, of which 6 were waited for; matrix products, arithmetic and copies ran while one was open for 2% of the time, Pallas kernels for 0%

commit v1 on v0

v1 whole, which is shorter than its diff:
```python
import functools

import jax
import jax.numpy as jnp
from jax import lax
from jax.experimental import pallas as pl
from jax.experimental.pallas import tpu as pltpu
from jax.sharding import PartitionSpec as P


F32 = jnp.float32
BF16 = jnp.bfloat16
LOG2E = 1.4426950408889634
D = 1024
HID = 4096
TOK = 256
HALF = 128
OWN = 4
GRP = 16
VMEM_LIMIT = 66_000_000
NT = (((1,), (1,)), ((), ()))
TN = (((0,), (0,)), ((), ()))
PART = 2


def dot(a, b):
    return jnp.dot(a, b, preferred_element_type=F32)


def dot_nt(a, b):
    return lax.dot_general(a, b, NT, preferred_element_type=F32)


def norm_rows(xb):
    mean = jnp.mean(xb, axis=-1, keepdims=True)
    cen = xb - mean
    var = jnp.mean(cen * cen, axis=-1, keepdims=True)
    return cen * lax.rsqrt(var + 1e-6)


def norm_mod(src, src_row, dst, dst_row, shift, scale, rows, blk=32):
    gain = 1.0 + scale

    def body(i, carry):
        rs = pl.multiple_of(src_row + i * blk, blk)
        rd = pl.multiple_of(dst_row + i * blk, blk)
        dst[pl.ds(rd, blk), :] = (norm_rows(src[pl.ds(rs, blk), :]) * gain + shift).astype(BF16)
        return carry

    lax.fori_loop(0, rows // blk, body, 0)


def gelu(v):
    return v * (0.5 + 0.5 * jnp.tanh(v * (0.7978845608028654 + (0.7978845608028654 * 0.044715) * (v * v))))


def dot_tn(a, b):
    return lax.dot_general(a, b, TN, preferred_element_type=F32)


def softmax_bf16(t):
    top = jnp.max(t, axis=0, keepdims=True)
    e = jnp.exp2(t - top)
    return (e * (1.0 / jnp.sum(e, axis=0, keepdims=True))).astype(BF16)


def half_masks():
    lane = lax.broadcasted_iota(jnp.int32, (1, 128), 1)
    low = (lane < 64).astype(F32)
    return low.astype(BF16), (1.0 - low).astype(BF16), lane < 64


def dense_kernel(*refs, do_c, do_a, ns, layer, part):
    it = iter(refs)
    x_in = next(it)
    if do_c:
        o_keep, o_recv, mod_c, wto, wup, wdn = (next(it) for _ in range(6))
    if do_a:
        mod_a, wsqkv, wso = (next(it) for _ in range(3))
    x = next(it)
    if do_a:
        u_keep, u_send = next(it), next(it)
    u_buf, o_buf = next(it), next(it)
    if do_c:
        vto, vup, vdn, h_buf = (next(it) for _ in range(4))
    if do_a:
        vsqkv, vso, qkv_buf = (next(it) for _ in range(3))
    sems = next(it)

    rows = ns * TOK
    core = lax.rem(lax.axis_index('frames'), 2)
    copies = []
    if do_c:
        copies += [pltpu.make_async_copy(wto.at[layer], vto, sems.at[0]),
                   pltpu.make_async_copy(wup.at[layer], vup, sems.at[1]),
                   pltpu.make_async_copy(wdn.at[layer], vdn, sems.at[2])]
    nxt = layer + 1 if do_c else layer
    if do_a:
        copies += [pltpu.make_async_copy(wsqkv.at[nxt], vsqkv, sems.at[3]),
                   pltpu.make_async_copy(wso.at[nxt], vso, sems.at[4])]
    state = {'next': 0}

    def start_more():
        if state['next'] < len(copies):
            copies[state['next']].start()
            state['next'] += 1

    def arrive(k):
        copies[k].wait()
        start_more()

    start_more()
    start_more()
    k = 0
    if do_c:
        for s in range(ns):
            o_buf[pl.ds(pl.multiple_of(s * TOK + core * HALF, HALF), HALF), :] = o_keep[part * ns + s]
            o_buf[pl.ds(pl.multiple_of(s * TOK + (1 - core) * HALF, HALF), HALF), :] = o_recv[part * ns + s]
        arrive(0)

        def proj(j, carry):
            c = pl.ds(pl.multiple_of(j * 256, 256), 256)
            x[:, c] = x_in[:, c] + dot(o_buf[...], vto[:, c])
            return carry

        lax.fori_loop(0, D // 256, proj, 0)
        for s in range(ns):
            norm_mod(x, s * TOK, u_buf, s * TOK, mod_c[s, 4:5, :], mod_c[s, 5:6, :], TOK)
        arrive(1)
        hrows = min(rows, 512)
        for b in range(rows // hrows):
            rb = pl.ds(b * hrows, hrows)

            def up(j, carry):
                c = pl.ds(pl.multiple_of(j * 256, 256), 256)
                h_buf[:, c] = gelu(dot(u_buf[rb, :], vup[:, c])).astype(BF16)
                return carry

            lax.fori_loop(0, HID // 256, up, 0)
            if b == 0:
                arrive(2)

            def down(j, carry):
                c = pl.ds(pl.multiple_of(j * 256, 256), 256)
                x[rb, c] = x[rb, c] + dot(h_buf[...], vdn[:, c])
                return carry

            lax.fori_loop(0, D // 256, down, 0)
        k = 3
    else:
        x[...] = x_in[...]
    if do_a:
        for s in range(ns):
            norm_mod(x, s * TOK, u_buf, s * TOK, mod_a[s, 0:1, :], mod_a[s, 1:2, :], TOK)
        arrive(k)

        def qkv(j, carry):
            c = pl.ds(pl.multiple_of(j * 256, 256), 256)
            qkv_buf[:, c] = dot_nt(u_buf[...], vsqkv[c, :]).astype(BF16)
            return carry

        lax.fori_loop(0, 3 * D // 256, qkv, 0)
        low, high, is_low = half_masks()

        def attend(i, carry):
            r = pl.ds(pl.multiple_of((i // 2) * TOK, TOK), TOK)
            for h in range(4):
                c = (i % 2) * 512 + h * 128
                q = qkv_buf[r, pl.ds(pl.multiple_of(c, 128), 128)]
                key = qkv_buf[r, pl.ds(pl.multiple_of(D + c, 128), 128)]
                val = qkv_buf[r, pl.ds(pl.multiple_of(2 * D + c, 128), 128)]
                both = jnp.concatenate([q * low, q * high], axis=0)
                mixed = dot_tn(softmax_bf16(dot_nt(key, both) * (0.125 * LOG2E)), val)
                o_buf[r, pl.ds(pl.multiple_of(c, 128), 128)] = jnp.where(is_low, mixed[:TOK], mixed[TOK:]).astype(BF16)
            return carry

        lax.fori_loop(0, ns * 2, attend, 0)
        arrive(k + 1)

        def proj_s(j, carry):
            c = pl.ds(pl.multiple_of(j * 256, 256), 256)
            x[:, c] = x[:, c] + dot(o_buf[...], vso[:, c])
            return carry

        lax.fori_loop(0, D // 256, proj_s, 0)
        for s in range(ns):
            norm_mod(x, s * TOK + core * HALF, u_keep.at[s], 0, mod_a[s, 2:3, :], mod_a[s, 3:4, :], HALF)
            norm_mod(x, s * TOK + (1 - core) * HALF, u_send.at[s], 0, mod_a[s, 2:3, :], mod_a[s, 3:4, :], HALF)


VM = pl.BlockSpec(memory_space=pltpu.VMEM)
HB = pl.BlockSpec(memory_space=pl.ANY)


def dense_call(layer, part, do_c, do_a, x, c_args, a_args):
    rows = x.shape[0]
    ns = rows // TOK
    args, specs = [x], [VM]
    if do_c:
        args += c_args
        specs += [VM, VM, VM, HB, HB, HB]
    if do_a:
        args += a_args
        specs += [VM, HB, HB]
    outs = [jax.ShapeDtypeStruct((rows, D), F32)]
    if do_a:
        outs += [jax.ShapeDtypeStruct((ns, HALF, D), BF16)] * 2
    scratch = [pltpu.VMEM((rows, D), BF16), pltpu.VMEM((rows, D), BF16)]
    if do_c:
        scratch += [pltpu.VMEM((D, D), BF16), pltpu.VMEM((D, HID), BF16), pltpu.VMEM((HID, D), BF16),
                    pltpu.VMEM((min(rows, 512), HID), BF16)]
    if do_a:
        scratch += [pltpu.VMEM((3 * D, D), BF16), pltpu.VMEM((D, D), BF16), pltpu.VMEM((rows, 3 * D), BF16)]
    scratch.append(pltpu.SemaphoreType.DMA((5,)))
    flops = 2 * rows * D * ((D + 2 * HID) * do_c + 4 * D * do_a)
    return pl.pallas_call(
        functools.partial(dense_kernel, do_c=do_c, do_a=do_a, ns=ns, layer=layer, part=part),
        out_shape=outs,
        in_specs=specs,
        out_specs=[VM] * len(outs),
        scratch_shapes=scratch,
        compiler_params=pltpu.CompilerParams(vmem_limit_bytes=VMEM_LIMIT),
        cost_estimate=pl.CostEstimate(flops=flops, bytes_accessed=rows * D * 8, transcendentals=0),
        name='dense',
    )(*args)


def own_kernel(*refs, layer):
    keeps, swaps = refs[:OWN // PART], refs[OWN // PART:2 * OWN // PART]
    wqkv, q, kv, u_buf, w_buf, sem = refs[2 * OWN // PART:]
    core = lax.rem(lax.axis_index('frames'), 2)
    copy = pltpu.make_async_copy(wqkv.at[layer], w_buf, sem)
    copy.start()
    for s in range(OWN):
        u_buf[pl.ds(pl.multiple_of((core * OWN + s) * HALF, HALF), HALF), :] = keeps[s // PART][s % PART]
        u_buf[pl.ds(pl.multiple_of(((1 - core) * OWN + s) * HALF, HALF), HALF), :] = swaps[s // PART][s % PART]
    copy.wait()

    def q_part(j, carry):
        c = pl.ds(pl.multiple_of(j * 256, 256), 256)
        q[:, :, c] = dot_nt(u_buf[...], w_buf[c, :]).astype(BF16).reshape(2 * OWN, HALF, 256)
        return carry

    lax.fori_loop(0, D // 256, q_part, 0)

    def kv_part(j, carry):
        c = pl.ds(pl.multiple_of(j * 256, 256), 256)
        w = w_buf[pl.ds(pl.multiple_of(D + j * 256, 256), 256), :]
        kv[:, :, c] = dot_nt(u_buf[...], w).astype(BF16).reshape(2 * OWN, HALF, 256)
        return carry

    lax.fori_loop(0, 2 * D // 256, kv_part, 0)


def own_call(layer, keeps, swaps, w_tqkv):
    rows = 2 * OWN * HALF
    return pl.pallas_call(
        functools.partial(own_kernel, layer=layer),
        out_shape=[jax.ShapeDtypeStruct((2 * OWN, HALF, D), BF16), jax.ShapeDtypeStruct((2 * OWN, HALF, 2 * D), BF16)],
        in_specs=[VM] * (2 * OWN // PART) + [HB],
        out_specs=[VM, VM],
        scratch_shapes=[pltpu.VMEM((rows, D), BF16), pltpu.VMEM((3 * D, D), BF16), pltpu.SemaphoreType.DMA],
        compiler_params=pltpu.CompilerParams(vmem_limit_bytes=VMEM_LIMIT),
        cost_estimate=pl.CostEstimate(flops=6 * rows * D * D, bytes_accessed=16 << 20, transcendentals=0),
        name='temporal_own',
    )(*keeps, *swaps, w_tqkv)


def halo_kernel(*refs, layer):
    n = OWN // PART
    q, kv_own = refs[:2]
    near_k, near_s, up_k, up_s, down_k, down_s = (refs[2 + n * i:2 + n * i + n] for i in range(6))
    bias_all, wqkv, o_keep, o_send, u_buf, kv, bias, w_buf, o_buf, sems, halo_sems = refs[2 + 6 * n:]
    pos = lax.axis_index('frames')
    core = lax.rem(pos, 2)
    other = 1 - core
    row = pos // 2
    cw = pltpu.make_async_copy(wqkv.at[layer, pl.ds(D, 2 * D)], w_buf, sems.at[0])
    cw.start()

    def into(src, slot, k):
        return [pltpu.make_async_copy(src[i], u_buf.at[pl.ds(slot + PART * i, PART)], halo_sems.at[k, i]) for i in range(n)]

    near = into(near_k, core * OWN, 0) + into(near_s, other * OWN, 1)
    up = into(up_k, (2 + core) * OWN, 2) + into(up_s, (2 + other) * OWN, 3)
    down = into(down_k, (2 + core) * OWN, 2) + into(down_s, (2 + other) * OWN, 3)
    for c in near:
        c.start()

    @pl.when(row == 1)
    def _():
        for c in up:
            c.start()

    @pl.when(row == 0)
    def _():
        for c in down:
            c.start()

    c4 = pltpu.make_async_copy(kv_own, kv.at[pl.ds(4 * OWN, 2 * OWN)], sems.at[1])
    c4.start()
    c5 = pltpu.make_async_copy(bias_all.at[layer], bias, sems.at[2])
    c5.start()
    for c in [cw] + near + up:
        c.wait()

    def fill(i, carry):
        s = (i // 8) * 4
        j = i % 8
        c = pl.ds(pl.multiple_of(j * 256, 256), 256)
        a = u_buf[pl.ds(s, 4)].reshape(4 * HALF, D)
        kv[pl.ds(s, 4), :, c] = dot_nt(a, w_buf[c, :]).astype(BF16).reshape(4, HALF, 256)
        return carry

    lax.fori_loop(0, 32, fill, 0)
    c4.wait()
    c5.wait()
    low, high, is_low = half_masks()

    def attend(i, carry):
        tok = pl.ds(pl.multiple_of(i * GRP, GRP), GRP)
        for hp in range(8):
            c = slice(hp * 128, hp * 128 + 128)
            qb = q[:, tok, c].reshape(2 * OWN * GRP, 128)
            key = kv[:, tok, c].reshape(6 * OWN * GRP, 128)
            val = kv[:, tok, D + hp * 128:D + hp * 128 + 128].reshape(6 * OWN * GRP, 128)
            mixed = []
            for e, m in enumerate((low, high)):
                t = dot_nt(key, qb * m) * (0.125 * LOG2E) + bias[2 * hp + e]
                mixed.append(dot_tn(softmax_bf16(t), val))
            o = jnp.where(is_low, mixed[0], mixed[1]).astype(BF16)
            o_buf[:, tok, c] = o.reshape(2 * OWN, GRP, 128)
        return carry

    lax.fori_loop(0, HALF // GRP, attend, 0)
    o_keep[...] = o_buf[pl.ds(core * OWN, OWN)]
    o_send[...] = o_buf[pl.ds(other * OWN, OWN)]


def halo_call(layer, q, kv_own, halos, bias, w_tqkv):
    n = 2 * OWN
    return pl.pallas_call(
        functools.partial(halo_kernel, layer=layer),
        out_shape=[jax.ShapeDtypeStruct((OWN, HALF, D), BF16)] * 2,
        in_specs=[VM] + [HB] * (3 + len(halos)),
        out_specs=[VM, VM],
        scratch_shapes=[pltpu.VMEM((2 * n, HALF, D), BF16), pltpu.VMEM((3 * n, HALF, 2 * D), BF16),
                        pltpu.VMEM((16, 3 * n * GRP, n * GRP), F32), pltpu.VMEM((2 * D, D), BF16),
                        pltpu.VMEM((n, HALF, D), BF16), pltpu.SemaphoreType.DMA((3,)),
                        pltpu.SemaphoreType.DMA((4, OWN // PART))],
        compiler_params=pltpu.CompilerParams(vmem_limit_bytes=VMEM_LIMIT),
        cost_estimate=pl.CostEstimate(flops=16 * n * HALF * D * D, bytes_accessed=16 << 20, transcendentals=0),
        name='temporal_halo',
    )(q, kv_own, *halos, bias, w_tqkv)


def bias_kernel(lag, out):
    base = 16 * (16 * lax.axis_index('tokens') + 8 * (lax.axis_index('frames') // 2))
    shape = out.shape[2:]
    col = lax.broadcasted_iota(jnp.int32, shape, 0)
    row = lax.broadcasted_iota(jnp.int32, shape, 1)
    gap = jnp.where(col + base >= 256, row + 256 - col, -1)
    layer = pl.program_id(0)

    def head(h, carry):
        acc = jnp.full(shape, -1e30, F32)
        for r in range(16):
            acc = jnp.where(gap == GRP * r, lag[layer, h, r] * LOG2E, acc)
        out[0, h] = acc
        return carry

    lax.fori_loop(0, 16, head, 0)


def bias_call(lag_bias):
    shape = (3, 16, 6 * OWN * GRP, 2 * OWN * GRP)
    return pl.pallas_call(
        bias_kernel,
        grid=(3,),
        out_shape=jax.ShapeDtypeStruct(shape, F32),
        in_specs=[pl.BlockSpec(memory_space=pltpu.SMEM)],
        out_specs=pl.BlockSpec((1,) + shape[1:], lambda i: (i, 0, 0, 0)),
        name='bias_table',
    )(lag_bias)


def solution(mesh):
    nz = mesh.shape['tokens']
    slot_spec = P(('videos', 'frames'), 'tokens', None)
    mod_spec = P(('videos', 'frames'), None, None, None)
    step_spec = P(('videos', 'frames'))
    noise_spec = P('videos', 'tokens', None)
    emit_spec = P('videos', ('tokens', 'frames'), None)
    group = ('tokens', 'frames')
    same = [(z * 4 + f, (z + 1) * 4 + f) for z in range(nz - 1) for f in range(4)]
    cross = [(z * 4 + f, (z + 1) * 4 + (f ^ 1)) for z in range(nz - 1) for f in range(4)]

    def body(z_loc, mod_loc, step_loc, noise_loc, lag_bias, w_in, w_out, w_sqkv, w_so, w_tqkv, w_to, w_up, w_down):
        zc = lax.axis_index('tokens')
        fc = lax.axis_index('frames')
        layers = w_up.shape[0]
        n_steps = noise_loc.shape[0]
        sq = jnp.transpose(w_sqkv, (0, 2, 3, 4, 1)).reshape(layers, 3 * D, D)
        tq = jnp.transpose(w_tqkv, (0, 2, 3, 4, 1)).reshape(layers, 3 * D, D)
        so = w_so.reshape(layers, D, D)
        to = w_to.reshape(layers, D, D)
        bias = bias_call(lag_bias)

        small = jnp.concatenate([z_loc.reshape(16, 256), noise_loc.reshape(n_steps, 256),
                                 jnp.pad(step_loc, (0, 240))[None]], axis=0)
        small = lax.all_gather(small, group, axis=0).reshape(nz, 4, 17 + n_steps, 256)
        z_all = small[:, :, :16].reshape(nz, 4, 16, 64, 4).transpose(1, 2, 0, 3, 4).reshape(64, TOK * 4)
        noise = small[:, 0, 16:16 + n_steps].reshape(nz, n_steps, 256).transpose(1, 0, 2).reshape(n_steps, TOK * 4)
        first = 16 * zc + 4 * fc
        dt = lax.dynamic_slice(small[0, :, 16 + n_steps, :16].reshape(64), (first,), (4,))
        mod = lax.all_to_all(mod_loc.reshape(4, 4, layers, 6, D), 'frames', 0, 0)
        mod = lax.dynamic_index_in_dim(mod, zc, 0, keepdims=False)
        mods = [[mod[p * PART:(p + 1) * PART, l] for p in range(OWN // PART)] for l in range(layers)]

        def one_step(s, z_all):
            z_cur = lax.dynamic_slice(z_all, (first, 0), (4, TOK * 4)).reshape(4 * TOK, 4)
            x = dot(z_cur.astype(BF16), w_in).astype(BF16).astype(F32)
            parts = range(OWN // PART)
            rows = PART * TOK
            xs = [x[p * rows:(p + 1) * rows] for p in parts]
            c_args = None
            for l in range(layers):
                keeps, sends = [], []
                for p in parts:
                    ca = () if c_args is None else c_args + [mods[l - 1][p], to, w_up, w_down]
                    xs[p], keep, send = dense_call(l - 1 if l else 0, p, l > 0, True, xs[p], ca, [mods[l][p], sq, so])
                    keeps.append(keep)
                    sends.append(send)

                def move(vals, axes, pairs):
                    out = []
                    for p in parts:
                        out.append(lax.ppermute(vals[p], axes, pairs))
                    return out

                near_k = move(keeps, group, same)
                near_s = move(sends, group, cross)
                up_k = move(keeps, 'frames', [(0, 2), (1, 3)])
                up_s = move(sends, 'frames', [(0, 3), (1, 2)])
                swaps = move(sends, 'frames', [(0, 1), (1, 0), (2, 3), (3, 2)])
                down_k = move(near_k, 'frames', [(2, 0), (3, 1)])
                down_s = move(near_s, 'frames', [(2, 0), (3, 1)])
                q, kv_own = own_call(l, keeps, swaps, tq)
                halos = near_k + near_s + up_k + up_s + down_k + down_s
                o_keep, o_send = halo_call(l, q, kv_own, halos, bias, tq)
                o_recv = lax.ppermute(o_send, 'frames', [(0, 1), (1, 0), (2, 3), (3, 2)])
                c_args = [o_keep, o_recv]
            xs = [dense_call(layers - 1, p, True, False, xs[p], c_args + [mods[layers - 1][p], to, w_up, w_down], ())[0]
                  for p in parts]
            x = jnp.concatenate(xs, axis=0)
            vel = dot(norm_rows(x).astype(BF16), w_out)
            z_new = (z_cur + jnp.repeat(dt, TOK)[:, None] * vel).reshape(4, TOK * 4)
            z_new = lax.all_gather(z_new, group, axis=0, tiled=True)
            emit = lax.dynamic_slice(z_new[0].reshape(TOK, 4), (64 * zc + 16 * fc, 0), (16, 4))
            return jnp.concatenate([z_new[1:], noise[s][None]], axis=0), emit

        emits = []
        for s in range(n_steps):
            z_all, emit = one_step(s, z_all)
            emits.append(emit)
        z_out = lax.dynamic_slice(z_all.reshape(64, TOK, 4), (16 * fc, 64 * zc, 0), (16, 64, 4))
        return jnp.stack(emits), z_out

    return jax.shard_map(body, mesh=mesh, in_specs=(slot_spec, mod_spec, step_spec, noise_spec) + (P(),) * 9,
                         out_specs=(emit_spec, slot_spec), check_vma=False)
```

time: 3340 us -> 1470 us (0.44)
  matrix products: 900 us -> 3.06 us
  Pallas kernels: 0 us -> 844 us
  blocking collectives: 846 us -> 70.8 us
  local copies, waits for them, and re-layouts: 744 us -> 30.7 us
  other arithmetic: 303 us -> 7.26 us
  starting transfers between devices: 312 us -> 158 us
  waiting for transfers between devices: 202 us -> 345 us
    dot_general x58 -> x4, matrix products: 900 us -> 3.06 us  [dot(): return jnp.dot(a, b, preferred_element_type=F32)]
    all_to_all x12 -> x0, blocking collectives: 846 us -> none  [the longest x6 605 us: spatial_block(): qkv_full = lax.all_to_all(qkv_loc, 'tokens', 3, 1, tiled=True)]
    pallas_call x0 -> x29, Pallas kernels: none -> 844 us  [the longest x16 513 us: dense_call(): pl.pallas_call(functools.partial(dense_kernel, do_c=do_c, do_a=do_a, ns=n...]
    while x203 -> x0, local copies, waits for them, and re-layouts: 274 us -> none
    all_to_all x18 -> x0, local copies, waits for them, and re-layouts: 273 us -> none  [the longest x12 230 us: spatial_block(): qkv_full = lax.all_to_all(qkv_loc, 'tokens', 3, 1, tiled=True)]
    sub x14 -> x0, other arithmetic: 195 us -> none  [the longest x6 114 us: spatial_block(): attn_prob = jax.nn.softmax(scores, axis=-1).astype(jnp.bfloat16)]
    ppermute x8 -> x90, waiting for transfers between devices: 161 us -> 345 us  [the longest x84 331 us: move(): out.append(lax.ppermute(vals[p], axes, pairs))]
    ppermute x8 -> x90, starting transfers between devices: 311 us -> 153 us  [the longest x84 153 us: move(): out.append(lax.ppermute(vals[p], axes, pairs))]
  transfers between devices with their start and end apart: 10 -> 91, of which waited for: 6 -> 47; matrix products, arithmetic and copies ran while one was open for 2% -> 1% of each run, Pallas kernels for 0% -> 20%
where the time goes in v1:
time: 1470 us; the launch traced here: 1460 us
  Pallas kernels  844 us (57%)
  waiting for transfers between devices  345 us (23%)
  starting transfers between devices  158 us (11%)
  blocking collectives  70.8 us (5%)
  local copies, waits for them, and re-layouts  30.7 us (2%)
    pallas_call x16, Pallas kernels, dense_call(): pl.pallas_call(functools.partial(dense_kernel, do_c=do_c, do_a=do_a, ns=n...  513 us
    ppermute x84, waiting for transfers between devices, move(): out.append(lax.ppermute(vals[p], axes, pairs))  331 us
    pallas_call x6, Pallas kernels, halo_call(): pl.pallas_call(functools.partial(halo_kernel, layer=layer), out_shape=[ja...  226 us
    ppermute x84, starting transfers between devices, move(): out.append(lax.ppermute(vals[p], axes, pairs))  153 us
    pallas_call x6, Pallas kernels, own_call(): pl.pallas_call(functools.partial(own_kernel, layer=layer), out_shape=[jax...  91.9 us
    all_gather x2, blocking collectives, one_step(): z_new = lax.all_gather(z_new, group, axis=0, tiled=True)  38.5 us
    all_gather x1, blocking collectives, body(): lax.all_gather(small, group, axis=0).reshape(nz, 4, 17 + n_steps, 256)  32.3 us
  transfers between devices with their start and end apart: 91, of which 47 were waited for; matrix products, arithmetic and copies ran while one was open for 1% of the time, Pallas kernels for 20%

profile of v1, /device:TPU:0, one launch (start us, length us, event | category | flops | bytes accessed | tf_op | source)
XLA Modules:
  0.0 1460.3 jit_solution(16917526420258663312)
XLA Ops:
  8.3 32.3 %all-gather.1 = f32[16,19,256]{2,1,0:T(8,128)S(1)} all-gather(f32[1,19,256]{2,1,0:T(8,128)S(1)} %maximum_bitcast_fusion), channel_id=2, replica_groups=mesh['videos'=2,'tokens'=4,'frames'=4] {'tokens','frames'}, dimensions={0}, use_global_device_ids=true | all-gather | bytes 330752 | tf_op jit(solution)/shard_map/all_gather | solution.py:411
  52.4 21.7 %dense.16 = (f32[512,1024]{1,0:T(8,128)}, bf16[2,128,1024]{2,1,0:T(8,128)(2,1)}, bf16[2,128,1024]{2,1,0:T(8,128)(2,1)}) custom-call(f32[512,1024]{1,0:T(8,128)} %get-tuple-element.132.refs_0_, f32[2,6,1024]{2,1,0:T(8,128)} %get-tuple-element.139.refs_1_.refs_3_, bf16[3,3072,1024]{2,1,0:T(8,128)(2,1)} %bitcast.59, bf16[3,1024,1024]{2,1,0:T(8,128)(2,1)} %bitcast.83), custom_call_target="tpu_custom_call" | custom-call | flops 4294967296 | bytes 4194304 | tf_op jit(solution)/shard_map/dense/pallas_call | solution.py:216
  74.5 21.8 %dense.17 = (f32[512,1024]{1,0:T(8,128)}, bf16[2,128,1024]{2,1,0:T(8,128)(2,1)}, bf16[2,128,1024]{2,1,0:T(8,128)(2,1)}) custom-call(f32[512,1024]{1,0:T(8,128)} %get-tuple-element.133.refs_0_, f32[2,6,1024]{2,1,0:T(8,128)} %get-tuple-element.138.refs_1_.refs_3_, bf16[3,3072,1024]{2,1,0:T(8,128)(2,1)} %bitcast.60, bf16[3,1024,1024]{2,1,0:T(8,128)(2,1)} %bitcast.84), custom_call_target="tpu_custom_call" | custom-call | flops 4294967296 | bytes 4194304 | tf_op jit(solution)/shard_map/dense/pallas_call | solution.py:216
  193.1 37.6 %temporal_halo.6 = (bf16[4,128,1024]{2,1,0:T(8,128)(2,1)}, bf16[4,128,1024]{2,1,0:T(8,128)(2,1)}) custom-call(bf16[8,128,1024]{2,1,0:T(8,128)(2,1)} %get-tuple-element.67.refs_0_, bf16[8,128,2048]{2,1,0:T(8,128)(2,1)} %get-tuple-element.68.refs_1_, bf16[2,128,1024]{2,1,0:T(8,128)(2,1)} %copy-done.19, bf16[2,128,1024]{2,1,0:T(8,128)(2,1)} %collective-permute-done.3.refs_3_, ...), custom_call_target="tpu_custom_call" | custom-call | flops 17179869184 | bytes 16777216 | tf_op jit(solution)/shard_map/temporal_halo/pallas_call | solution.py:342
  233.7 41.7 %dense.18 = (f32[512,1024]{1,0:T(8,128)}, bf16[2,128,1024]{2,1,0:T(8,128)(2,1)}, bf16[2,128,1024]{2,1,0:T(8,128)(2,1)}) custom-call(f32[512,1024]{1,0:T(8,128)} %get-tuple-element.62.refs_0_, bf16[4,128,1024]{2,1,0:T(8,128)(2,1)} %get-tuple-element.69.refs_1_, bf16[4,128,1024]{2,1,0:T(8,128)(2,1)} %collective-permute-done.14.refs_2_, ...), custom_call_target="tpu_custom_call" | custom-call | flops 13958643712 | bytes 4194304 | tf_op jit(solution)/shard_map/dense/pallas_call | solution.py:216
  275.7 41.7 %dense.19 = (f32[512,1024]{1,0:T(8,128)}, bf16[2,128,1024]{2,1,0:T(8,128)(2,1)}, bf16[2,128,1024]{2,1,0:T(8,128)(2,1)}) custom-call(f32[512,1024]{1,0:T(8,128)} %get-tuple-element.73.refs_0_, bf16[4,128,1024]{2,1,0:T(8,128)(2,1)} %get-tuple-element.69.refs_1_, bf16[4,128,1024]{2,1,0:T(8,128)(2,1)} %collective-permute-done.14.refs_2_, ...), custom_call_target="tpu_custom_call" | custom-call | flops 13958643712 | bytes 4194304 | tf_op jit(solution)/shard_map/dense/pallas_call | solution.py:216
  416.5 37.6 %temporal_halo.7 = (bf16[4,128,1024]{2,1,0:T(8,128)(2,1)}, bf16[4,128,1024]{2,1,0:T(8,128)(2,1)}) custom-call(bf16[8,128,1024]{2,1,0:T(8,128)(2,1)} %get-tuple-element.77.refs_0_, bf16[8,128,2048]{2,1,0:T(8,128)(2,1)} %get-tuple-element.78.refs_1_, bf16[2,128,1024]{2,1,0:T(8,128)(2,1)} %copy-done.23, bf16[2,128,1024]{2,1,0:T(8,128)(2,1)} %collective-permute-done.18.refs_3_, ...), custom_call_target="tpu_custom_call" | custom-call | flops 17179869184 | bytes 16777216 | tf_op jit(solution)/shard_map/temporal_halo/pallas_call | solution.py:342
  457.2 41.7 %dense.20 = (f32[512,1024]{1,0:T(8,128)}, bf16[2,128,1024]{2,1,0:T(8,128)(2,1)}, bf16[2,128,1024]{2,1,0:T(8,128)(2,1)}) custom-call(f32[512,1024]{1,0:T(8,128)} %get-tuple-element.71.refs_0_, bf16[4,128,1024]{2,1,0:T(8,128)(2,1)} %get-tuple-element.79.refs_1_, bf16[4,128,1024]{2,1,0:T(8,128)(2,1)} %collective-permute-done.29.refs_2_, ...), custom_call_target="tpu_custom_call" | custom-call | flops 13958643712 | bytes 4194304 | tf_op jit(solution)/shard_map/dense/pallas_call | solution.py:216
  499.1 41.8 %dense.21 = (f32[512,1024]{1,0:T(8,128)}, bf16[2,128,1024]{2,1,0:T(8,128)(2,1)}, bf16[2,128,1024]{2,1,0:T(8,128)(2,1)}) custom-call(f32[512,1024]{1,0:T(8,128)} %get-tuple-element.83.refs_0_, bf16[4,128,1024]{2,1,0:T(8,128)(2,1)} %get-tuple-element.79.refs_1_, bf16[4,128,1024]{2,1,0:T(8,128)(2,1)} %collective-permute-done.29.refs_2_, ...), custom_call_target="tpu_custom_call" | custom-call | flops 13958643712 | bytes 4194304 | tf_op jit(solution)/shard_map/dense/pallas_call | solution.py:216
  640.6 37.6 %temporal_halo.8 = (bf16[4,128,1024]{2,1,0:T(8,128)(2,1)}, bf16[4,128,1024]{2,1,0:T(8,128)(2,1)}) custom-call(bf16[8,128,1024]{2,1,0:T(8,128)(2,1)} %get-tuple-element.87.refs_0_, bf16[8,128,2048]{2,1,0:T(8,128)(2,1)} %get-tuple-element.88.refs_1_, bf16[2,128,1024]{2,1,0:T(8,128)(2,1)} %collective-permute-done.32.refs_2_, ...), custom_call_target="tpu_custom_call" | custom-call | flops 17179869184 | bytes 16777216 | tf_op jit(solution)/shard_map/temporal_halo/pallas_call | solution.py:342
  681.3 23.0 %dense.23 = f32[512,1024]{1,0:T(8,128)} custom-call(f32[512,1024]{1,0:T(8,128)} %get-tuple-element.91.refs_0_, bf16[4,128,1024]{2,1,0:T(8,128)(2,1)} %get-tuple-element.89.refs_1_, bf16[4,128,1024]{2,1,0:T(8,128)(2,1)} %collective-permute-done.44.refs_2_, f32[2,6,1024]{2,1,0:T(8,128)} %get-tuple-element.135.refs_7_.refs_3_, bf16[3,1024,1024]{2,1,0:T(8,128)(2,1)} %bitcast.75, ...), custom_call_target="tpu_custom_call" | custom-call | flops 9663676416 | bytes 4194304 | tf_op jit(solution)/shard_map/dense/pallas_call | solution.py:216
  704.3 23.1 %dense.22 = f32[512,1024]{1,0:T(8,128)} custom-call(f32[512,1024]{1,0:T(8,128)} %get-tuple-element.81.refs_0_, bf16[4,128,1024]{2,1,0:T(8,128)(2,1)} %get-tuple-element.89.refs_1_, bf16[4,128,1024]{2,1,0:T(8,128)(2,1)} %collective-permute-done.44.refs_2_, f32[2,6,1024]{2,1,0:T(8,128)} %get-tuple-element.134.refs_7_.refs_3_, bf16[3,1024,1024]{2,1,0:T(8,128)(2,1)} %bitcast.76, ...), custom_call_target="tpu_custom_call" | custom-call | flops 9663676416 | bytes 4194304 | tf_op jit(solution)/shard_map/dense/pallas_call | solution.py:216
  733.1 19.2 %all-gather.2 = f32[16,4,1024]{2,1,0:T(4,128)S(1)} all-gather(f32[1,4,1024]{2,1,0:T(4,128)S(1)} %reshape.96), channel_id=1, replica_groups=mesh['videos'=2,'tokens'=4,'frames'=4] {'tokens','frames'}, dimensions={0}, use_global_device_ids=true | all-gather | bytes 278528 | tf_op jit(solution)/shard_map/all_gather | solution.py:458
  756.8 21.7 %dense.25 = (f32[512,1024]{1,0:T(8,128)}, bf16[2,128,1024]{2,1,0:T(8,128)(2,1)}, bf16[2,128,1024]{2,1,0:T(8,128)(2,1)}) custom-call(f32[512,1024]{1,0:T(8,128)} %get-tuple-element.131.refs_0_, f32[2,6,1024]{2,1,0:T(8,128)} %get-tuple-element.138.refs_1_.refs_3_, bf16[3,3072,1024]{2,1,0:T(8,128)(2,1)} %bitcast.65, bf16[3,1024,1024]{2,1,0:T(8,128)(2,1)} %bitcast.89), custom_call_target="tpu_custom_call" | custom-call | flops 4294967296 | bytes 4194304 | tf_op jit(solution)/shard_map/dense/pallas_call | solution.py:216
  778.6 21.8 %dense.24 = (f32[512,1024]{1,0:T(8,128)}, bf16[2,128,1024]{2,1,0:T(8,128)(2,1)}, bf16[2,128,1024]{2,1,0:T(8,128)(2,1)}) custom-call(f32[512,1024]{1,0:T(8,128)} %get-tuple-element.130.refs_0_, f32[2,6,1024]{2,1,0:T(8,128)} %get-tuple-element.139.refs_1_.refs_3_, bf16[3,3072,1024]{2,1,0:T(8,128)(2,1)} %bitcast.66, bf16[3,1024,1024]{2,1,0:T(8,128)(2,1)} %bitcast.90), custom_call_target="tpu_custom_call" | custom-call | flops 4294967296 | bytes 4194304 | tf_op jit(solution)/shard_map/dense/pallas_call | solution.py:216
  897.6 37.6 %temporal_halo.9 = (bf16[4,128,1024]{2,1,0:T(8,128)(2,1)}, bf16[4,128,1024]{2,1,0:T(8,128)(2,1)}) custom-call(bf16[8,128,1024]{2,1,0:T(8,128)(2,1)} %get-tuple-element.97.refs_0_, bf16[8,128,2048]{2,1,0:T(8,128)(2,1)} %get-tuple-element.98.refs_1_, bf16[2,128,1024]{2,1,0:T(8,128)(2,1)} %collective-permute-done.47.refs_2_, ...), custom_call_target="tpu_custom_call" | custom-call | flops 17179869184 | bytes 16777216 | tf_op jit(solution)/shard_map/temporal_halo/pallas_call | solution.py:342
  938.3 41.7 %dense.26 = (f32[512,1024]{1,0:T(8,128)}, bf16[2,128,1024]{2,1,0:T(8,128)(2,1)}, bf16[2,128,1024]{2,1,0:T(8,128)(2,1)}) custom-call(f32[512,1024]{1,0:T(8,128)} %get-tuple-element.92.refs_0_, bf16[4,128,1024]{2,1,0:T(8,128)(2,1)} %get-tuple-element.99.refs_1_, bf16[4,128,1024]{2,1,0:T(8,128)(2,1)} %collective-permute-done.59.refs_2_, ...), custom_call_target="tpu_custom_call" | custom-call | flops 13958643712 | bytes 4194304 | tf_op jit(solution)/shard_map/dense/pallas_call | solution.py:216
  980.2 41.8 %dense.27 = (f32[512,1024]{1,0:T(8,128)}, bf16[2,128,1024]{2,1,0:T(8,128)(2,1)}, bf16[2,128,1024]{2,1,0:T(8,128)(2,1)}) custom-call(f32[512,1024]{1,0:T(8,128)} %get-tuple-element.103.refs_0_, bf16[4,128,1024]{2,1,0:T(8,128)(2,1)} %get-tuple-element.99.refs_1_, bf16[4,128,1024]{2,1,0:T(8,128)(2,1)} %collective-permute-done.59.refs_2_, ...), custom_call_target="tpu_custom_call" | custom-call | flops 13958643712 | bytes 4194304 | tf_op jit(solution)/shard_map/dense/pallas_call | solution.py:216
  1121.3 37.6 %temporal_halo.10 = (bf16[4,128,1024]{2,1,0:T(8,128)(2,1)}, bf16[4,128,1024]{2,1,0:T(8,128)(2,1)}) custom-call(bf16[8,128,1024]{2,1,0:T(8,128)(2,1)} %get-tuple-element.107.refs_0_, bf16[8,128,2048]{2,1,0:T(8,128)(2,1)} %get-tuple-element.108.refs_1_, bf16[2,128,1024]{2,1,0:T(8,128)(2,1)} %collective-permute-done.62.refs_2_, ...), custom_call_target="tpu_custom_call" | custom-call | flops 17179869184 | bytes 16777216 | tf_op jit(solution)/shard_map/temporal_halo/pallas_call | solution.py:342
  1161.9 41.7 %dense.28 = (f32[512,1024]{1,0:T(8,128)}, bf16[2,128,1024]{2,1,0:T(8,128)(2,1)}, bf16[2,128,1024]{2,1,0:T(8,128)(2,1)}) custom-call(f32[512,1024]{1,0:T(8,128)} %get-tuple-element.101.refs_0_, bf16[4,128,1024]{2,1,0:T(8,128)(2,1)} %get-tuple-element.109.refs_1_, bf16[4,128,1024]{2,1,0:T(8,128)(2,1)} %collective-permute-done.74.refs_2_, ...), custom_call_target="tpu_custom_call" | custom-call | flops 13958643712 | bytes 4194304 | tf_op jit(solution)/shard_map/dense/pallas_call | solution.py:216
  1203.9 41.8 %dense.29 = (f32[512,1024]{1,0:T(8,128)}, bf16[2,128,1024]{2,1,0:T(8,128)(2,1)}, bf16[2,128,1024]{2,1,0:T(8,128)(2,1)}) custom-call(f32[512,1024]{1,0:T(8,128)} %get-tuple-element.113.refs_0_, bf16[4,128,1024]{2,1,0:T(8,128)(2,1)} %get-tuple-element.109.refs_1_, bf16[4,128,1024]{2,1,0:T(8,128)(2,1)} %collective-permute-done.74.refs_2_, ...), custom_call_target="tpu_custom_call" | custom-call | flops 13958643712 | bytes 4194304 | tf_op jit(solution)/shard_map/dense/pallas_call | solution.py:216
  1345.3 37.6 %temporal_halo.11 = (bf16[4,128,1024]{2,1,0:T(8,128)(2,1)}, bf16[4,128,1024]{2,1,0:T(8,128)(2,1)}) custom-call(bf16[8,128,1024]{2,1,0:T(8,128)(2,1)} %get-tuple-element.117.refs_0_, bf16[8,128,2048]{2,1,0:T(8,128)(2,1)} %get-tuple-element.118.refs_1_, bf16[2,128,1024]{2,1,0:T(8,128)(2,1)} %collective-permute-done.77.refs_2_, ...), custom_call_target="tpu_custom_call" | custom-call | flops 17179869184 | bytes 16777216 | tf_op jit(solution)/shard_map/temporal_halo/pallas_call | solution.py:342
  1386.0 23.0 %dense.31 = f32[512,1024]{1,0:T(8,128)} custom-call(f32[512,1024]{1,0:T(8,128)} %get-tuple-element.121.refs_0_, bf16[4,128,1024]{2,1,0:T(8,128)(2,1)} %get-tuple-element.119.refs_1_, bf16[4,128,1024]{2,1,0:T(8,128)(2,1)} %collective-permute-done.89.refs_2_, f32[2,6,1024]{2,1,0:T(8,128)} %get-tuple-element.135.refs_7_.refs_3_, ...), custom_call_target="tpu_custom_call" | custom-call | flops 9663676416 | bytes 4194304 | tf_op jit(solution)/shard_map/dense/pallas_call | solution.py:216
  1409.0 23.0 %dense.30 = f32[512,1024]{1,0:T(8,128)} custom-call(f32[512,1024]{1,0:T(8,128)} %get-tuple-element.111.refs_0_, bf16[4,128,1024]{2,1,0:T(8,128)(2,1)} %get-tuple-element.119.refs_1_, bf16[4,128,1024]{2,1,0:T(8,128)(2,1)} %collective-permute-done.89.refs_2_, f32[2,6,1024]{2,1,0:T(8,128)} %get-tuple-element.134.refs_7_.refs_3_, ...), custom_call_target="tpu_custom_call" | custom-call | flops 9663676416 | bytes 4194304 | tf_op jit(solution)/shard_map/dense/pallas_call | solution.py:216
  (343 shorter events, 667.9 us)
Async XLA Ops:
  3.5 46.9 %all-to-all-start = ((f32[4,4,3,6,1024]{4,1,3,2,0:T(4,128)}), f32[4,4,3,6,1024]{4,1,3,2,0:T(4,128)}, u32[]{:S(2)}, u32[]{:S(2)}) async-start(f32[4,4,3,6,1024]{4,1,3,2,0:T(4,128)} %copy.75), calls=%async_computation | async-start | bytes 2359296 | tf_op jit(solution)/shard_map/all_to_all | solution.py:416
  100.0 36.8 %collective-permute-start.4 = (bf16[2,128,1024]{2,1,0:T(8,128)(2,1)}, bf16[2,128,1024]{2,1,0:T(8,128)(2,1)}, u32[]{:S(2)}, u32[]{:S(2)}) collective-permute-start(bf16[2,128,1024]{2,1,0:T(8,128)(2,1)} %get-tuple-element.65), channel_id=1, source_target_pairs={{0,5},{1,4},{2,7},{3,6},{4,9},{5,8},{6,11},{7,10},{8,13},{9,12},{1... | collective-permute-start | bytes 1572872 | tf_op jit(solution)/shard_map/ppermute | solution.py:438
  102.6 41.2 %collective-permute-start.5 = (bf16[2,128,1024]{2,1,0:T(8,128)(2,1)}, bf16[2,128,1024]{2,1,0:T(8,128)(2,1)}, u32[]{:S(2)}, u32[]{:S(2)}) collective-permute-start(bf16[2,128,1024]{2,1,0:T(8,128)(2,1)} %get-tuple-element.66), channel_id=1, source_target_pairs={{0,5},{1,4},{2,7},{3,6},{4,9},{5,8},{6,11},{7,10},{8,13},{9,12},{1... | collective-permute-start | bytes 1572872 | tf_op jit(solution)/shard_map/ppermute | solution.py:438
  104.8 40.3 %collective-permute-start.6 = (bf16[2,128,1024]{2,1,0:T(8,128)(2,1)}, bf16[2,128,1024]{2,1,0:T(8,128)(2,1)}, u32[]{:S(2)}, u32[]{:S(2)}) collective-permute-start(bf16[2,128,1024]{2,1,0:T(8,128)(2,1)} %get-tuple-element.63.refs_0_), channel_id=1, source_target_pairs={{0,2},{1,3},{4,6},{5,7},{8,10},{9,11},{12,14},{13,15},{16,18},{17,... | collective-permute-start | bytes 1572872 | tf_op jit(solution)/shard_map/ppermute | solution.py:438
  147.7 45.3 %collective-permute-start.13 = (bf16[2,128,1024]{2,1,0:T(8,128)(2,1)}, bf16[2,128,1024]{2,1,0:T(8,128)(2,1)}, u32[]{:S(2)}, u32[]{:S(2)}) collective-permute-start(bf16[2,128,1024]{2,1,0:T(8,128)(2,1)} %collective-permute-done.5.refs_5_), channel_id=1, source_target_pairs={{2,0},{3,1},{6,4},{7,5},{10,8},{11,9},{14,12},{15,13},{18,16},{19,... | collective-permute-start | bytes 1572872 | tf_op jit(solution)/shard_map/ppermute | solution.py:438
  275.5 51.6 %collective-permute-start.15 = (bf16[2,128,1024]{2,1,0:T(8,128)(2,1)}, bf16[2,128,1024]{2,1,0:T(8,128)(2,1)}, u32[]{:S(2)}, u32[]{:S(2)}) collective-permute-start(bf16[2,128,1024]{2,1,0:T(8,128)(2,1)} %get-tuple-element.75), channel_id=1, source_target_pairs={{0,1},{1,0},{2,3},{3,2},{4,5},{5,4},{6,7},{7,6},{8,9},{9,8},{10,11... | collective-permute-start | bytes 1572872 | tf_op jit(solution)/shard_map/ppermute | solution.py:438
  327.1 40.6 %collective-permute-start.20 = (bf16[2,128,1024]{2,1,0:T(8,128)(2,1)}, bf16[2,128,1024]{2,1,0:T(8,128)(2,1)}, u32[]{:S(2)}, u32[]{:S(2)}) collective-permute-start(bf16[2,128,1024]{2,1,0:T(8,128)(2,1)} %get-tuple-element.76), channel_id=1, source_target_pairs={{0,5},{1,4},{2,7},{3,6},{4,9},{5,8},{6,11},{7,10},{8,13},{9,12},{1... | collective-permute-start | bytes 1572872 | tf_op jit(solution)/shard_map/ppermute | solution.py:438
  329.2 39.8 %collective-permute-start.21 = (bf16[2,128,1024]{2,1,0:T(8,128)(2,1)}, bf16[2,128,1024]{2,1,0:T(8,128)(2,1)}, u32[]{:S(2)}, u32[]{:S(2)}) collective-permute-start(bf16[2,128,1024]{2,1,0:T(8,128)(2,1)} %get-tuple-element.72.refs_0_), channel_id=1, source_target_pairs={{0,2},{1,3},{4,6},{5,7},{8,10},{9,11},{12,14},{13,15},{16,18},{17,... | collective-permute-start | bytes 1572872 | tf_op jit(solution)/shard_map/ppermute | solution.py:438
  372.1 44.5 %collective-permute-start.28 = (bf16[2,128,1024]{2,1,0:T(8,128)(2,1)}, bf16[2,128,1024]{2,1,0:T(8,128)(2,1)}, u32[]{:S(2)}, u32[]{:S(2)}) collective-permute-start(bf16[2,128,1024]{2,1,0:T(8,128)(2,1)} %collective-permute-done.20.refs_5_), channel_id=1, source_target_pairs={{2,0},{3,1},{6,4},{7,5},{10,8},{11,9},{14,12},{15,13},{18,16},{19,... | collective-permute-start | bytes 1572872 | tf_op jit(solution)/shard_map/ppermute | solution.py:438
  498.9 52.5 %collective-permute-start.30 = (bf16[2,128,1024]{2,1,0:T(8,128)(2,1)}, bf16[2,128,1024]{2,1,0:T(8,128)(2,1)}, u32[]{:S(2)}, u32[]{:S(2)}) collective-permute-start(bf16[2,128,1024]{2,1,0:T(8,128)(2,1)} %get-tuple-element.85), channel_id=1, source_target_pairs={{0,1},{1,0},{2,3},{3,2},{4,5},{5,4},{6,7},{7,6},{8,9},{9,8},{10,11... | collective-permute-start | bytes 1572872 | tf_op jit(solution)/shard_map/ppermute | solution.py:438
  551.4 40.2 %collective-permute-start.35 = (bf16[2,128,1024]{2,1,0:T(8,128)(2,1)}, bf16[2,128,1024]{2,1,0:T(8,128)(2,1)}, u32[]{:S(2)}, u32[]{:S(2)}) collective-permute-start(bf16[2,128,1024]{2,1,0:T(8,128)(2,1)} %get-tuple-element.86), channel_id=1, source_target_pairs={{0,5},{1,4},{2,7},{3,6},{4,9},{5,8},{6,11},{7,10},{8,13},{9,12},{1... | collective-permute-start | bytes 1572872 | tf_op jit(solution)/shard_map/ppermute | solution.py:438
  553.5 39.4 %collective-permute-start.36 = (bf16[2,128,1024]{2,1,0:T(8,128)(2,1)S(1)}, bf16[2,128,1024]{2,1,0:T(8,128)(2,1)S(1)}, u32[]{:S(2)}, u32[]{:S(2)}) collective-permute-start(bf16[2,128,1024]{2,1,0:T(8,128)(2,1)S(1)} %copy-done.24), channel_id=1, source_target_pairs={{0,2},{1,3},{4,6},{5,7},{8,10},{9,11},{12,14},{13,15},{16,18},{17,... | collective-permute-start | bytes 1572872 | tf_op jit(solution)/shard_map/ppermute | solution.py:438
  596.3 44.3 %collective-permute-start.43 = (bf16[2,128,1024]{2,1,0:T(8,128)(2,1)}, bf16[2,128,1024]{2,1,0:T(8,128)(2,1)}, u32[]{:S(2)}, u32[]{:S(2)}) collective-permute-start(bf16[2,128,1024]{2,1,0:T(8,128)(2,1)} %collective-permute-done.35.refs_5_), channel_id=1, source_target_pairs={{2,0},{3,1},{6,4},{7,5},{10,8},{11,9},{14,12},{15,13},{18,16},{19,... | collective-permute-start | bytes 1572872 | tf_op jit(solution)/shard_map/ppermute | solution.py:438
  807.3 40.8 %collective-permute-start.50 = (bf16[2,128,1024]{2,1,0:T(8,128)(2,1)S(1)}, bf16[2,128,1024]{2,1,0:T(8,128)(2,1)}, u32[]{:S(2)}, u32[]{:S(2)}) collective-permute-start(bf16[2,128,1024]{2,1,0:T(8,128)(2,1)S(1)} %copy-done.20), channel_id=1, source_target_pairs={{0,5},{1,4},{2,7},{3,6},{4,9},{5,8},{6,11},{7,10},{8,13},{9,12},{1... | collective-permute-start | bytes 1572872 | tf_op jit(solution)/shard_map/ppermute | solution.py:438
  809.4 40.0 %collective-permute-start.51 = (bf16[2,128,1024]{2,1,0:T(8,128)(2,1)}, bf16[2,128,1024]{2,1,0:T(8,128)(2,1)S(1)}, u32[]{:S(2)}, u32[]{:S(2)}) collective-permute-start(bf16[2,128,1024]{2,1,0:T(8,128)(2,1)} %get-tuple-element.93.refs_0_), channel_id=1, source_target_pairs={{0,2},{1,3},{4,6},{5,7},{8,10},{9,11},{12,14},{13,15},{16,18},{17,... | collective-permute-start | bytes 1572872 | tf_op jit(solution)/shard_map/ppermute | solution.py:438
  852.8 44.8 %collective-permute-start.58 = (bf16[2,128,1024]{2,1,0:T(8,128)(2,1)}, bf16[2,128,1024]{2,1,0:T(8,128)(2,1)}, u32[]{:S(2)}, u32[]{:S(2)}) collective-permute-start(bf16[2,128,1024]{2,1,0:T(8,128)(2,1)} %collective-permute-done.50.refs_5_), channel_id=1, source_target_pairs={{2,0},{3,1},{6,4},{7,5},{10,8},{11,9},{14,12},{15,13},{18,16},{19,... | collective-permute-start | bytes 1572872 | tf_op jit(solution)/shard_map/ppermute | solution.py:438
  980.0 51.9 %collective-permute-start.60 = (bf16[2,128,1024]{2,1,0:T(8,128)(2,1)}, bf16[2,128,1024]{2,1,0:T(8,128)(2,1)}, u32[]{:S(2)}, u32[]{:S(2)}) collective-permute-start(bf16[2,128,1024]{2,1,0:T(8,128)(2,1)} %get-tuple-element.105), channel_id=1, source_target_pairs={{0,1},{1,0},{2,3},{3,2},{4,5},{5,4},{6,7},{7,6},{8,9},{9,8},{10,11... | collective-permute-start | bytes 1572872 | tf_op jit(solution)/shard_map/ppermute | solution.py:438
  1031.9 40.3 %collective-permute-start.65 = (bf16[2,128,1024]{2,1,0:T(8,128)(2,1)}, bf16[2,128,1024]{2,1,0:T(8,128)(2,1)}, u32[]{:S(2)}, u32[]{:S(2)}) collective-permute-start(bf16[2,128,1024]{2,1,0:T(8,128)(2,1)} %get-tuple-element.106), channel_id=1, source_target_pairs={{0,5},{1,4},{2,7},{3,6},{4,9},{5,8},{6,11},{7,10},{8,13},{9,12},{1... | collective-permute-start | bytes 1572872 | tf_op jit(solution)/shard_map/ppermute | solution.py:438
  1034.0 39.7 %collective-permute-start.66 = (bf16[2,128,1024]{2,1,0:T(8,128)(2,1)S(1)}, bf16[2,128,1024]{2,1,0:T(8,128)(2,1)S(1)}, u32[]{:S(2)}, u32[]{:S(2)}) collective-permute-start(bf16[2,128,1024]{2,1,0:T(8,128)(2,1)S(1)} %copy-done.21), channel_id=1, source_target_pairs={{0,2},{1,3},{4,6},{5,7},{8,10},{9,11},{12,14},{13,15},{16,18},{17,... | collective-permute-start | bytes 1572872 | tf_op jit(solution)/shard_map/ppermute | solution.py:438
  1077.1 44.1 %collective-permute-start.73 = (bf16[2,128,1024]{2,1,0:T(8,128)(2,1)}, bf16[2,128,1024]{2,1,0:T(8,128)(2,1)}, u32[]{:S(2)}, u32[]{:S(2)}) collective-permute-start(bf16[2,128,1024]{2,1,0:T(8,128)(2,1)} %collective-permute-done.65.refs_5_), channel_id=1, source_target_pairs={{2,0},{3,1},{6,4},{7,5},{10,8},{11,9},{14,12},{15,13},{18,16},{19,... | collective-permute-start | bytes 1572872 | tf_op jit(solution)/shard_map/ppermute | solution.py:438
  1203.6 52.5 %collective-permute-start.75 = (bf16[2,128,1024]{2,1,0:T(8,128)(2,1)}, bf16[2,128,1024]{2,1,0:T(8,128)(2,1)}, u32[]{:S(2)}, u32[]{:S(2)}) collective-permute-start(bf16[2,128,1024]{2,1,0:T(8,128)(2,1)} %get-tuple-element.115), channel_id=1, source_target_pairs={{0,1},{1,0},{2,3},{3,2},{4,5},{5,4},{6,7},{7,6},{8,9},{9,8},{10,11... | collective-permute-start | bytes 1572872 | tf_op jit(solution)/shard_map/ppermute | solution.py:438
  1256.1 40.2 %collective-permute-start.80 = (bf16[2,128,1024]{2,1,0:T(8,128)(2,1)}, bf16[2,128,1024]{2,1,0:T(8,128)(2,1)}, u32[]{:S(2)}, u32[]{:S(2)}) collective-permute-start(bf16[2,128,1024]{2,1,0:T(8,128)(2,1)} %get-tuple-element.116), channel_id=1, source_target_pairs={{0,5},{1,4},{2,7},{3,6},{4,9},{5,8},{6,11},{7,10},{8,13},{9,12},{1... | collective-permute-start | bytes 1572872 | tf_op jit(solution)/shard_map/ppermute | solution.py:438
  1258.2 39.4 %collective-permute-start.81 = (bf16[2,128,1024]{2,1,0:T(8,128)(2,1)S(1)}, bf16[2,128,1024]{2,1,0:T(8,128)(2,1)S(1)}, u32[]{:S(2)}, u32[]{:S(2)}) collective-permute-start(bf16[2,128,1024]{2,1,0:T(8,128)(2,1)S(1)} %copy-done.22), channel_id=1, source_target_pairs={{0,2},{1,3},{4,6},{5,7},{8,10},{9,11},{12,14},{13,15},{16,18},{17,... | collective-permute-start | bytes 1572872 | tf_op jit(solution)/shard_map/ppermute | solution.py:438
  1301.0 44.3 %collective-permute-start.88 = (bf16[2,128,1024]{2,1,0:T(8,128)(2,1)}, bf16[2,128,1024]{2,1,0:T(8,128)(2,1)}, u32[]{:S(2)}, u32[]{:S(2)}) collective-permute-start(bf16[2,128,1024]{2,1,0:T(8,128)(2,1)} %collective-permute-done.80.refs_5_), channel_id=1, source_target_pairs={{2,0},{3,1},{6,4},{7,5},{10,8},{11,9},{14,12},{15,13},{18,16},{19,... | collective-permute-start | bytes 1572872 | tf_op jit(solution)/shard_map/ppermute | solution.py:438
  (111 other events, 2414.6 us)

commit v2 on v1

--- a/solution.py
+++ b/solution.py
@@ -38,7 +38,7 @@
     return cen * lax.rsqrt(var + 1e-6)
 
 
-def norm_mod(src, src_row, dst, dst_row, shift, scale, rows, blk=32):
+def norm_mod(src, src_row, dst, dst_row, shift, scale, rows, blk=128):
     gain = 1.0 + scale
 
     def body(i, carry):
@@ -225,52 +225,45 @@
     )(*args)
 
 
-def own_kernel(*refs, layer):
-    keeps, swaps = refs[:OWN // PART], refs[OWN // PART:2 * OWN // PART]
-    wqkv, q, kv, u_buf, w_buf, sem = refs[2 * OWN // PART:]
+def project_kernel(*refs, layer, start, cols):
+    n = OWN // PART
+    mine, theirs = refs[:n], refs[n:2 * n]
+    wqkv, out, u_buf, w_buf, sem = refs[2 * n:]
     core = lax.rem(lax.axis_index('frames'), 2)
-    copy = pltpu.make_async_copy(wqkv.at[layer], w_buf, sem)
+    copy = pltpu.make_async_copy(wqkv.at[layer, pl.ds(start, cols)], w_buf, sem)
     copy.start()
     for s in range(OWN):
-        u_buf[pl.ds(pl.multiple_of((core * OWN + s) * HALF, HALF), HALF), :] = keeps[s // PART][s % PART]
-        u_buf[pl.ds(pl.multiple_of(((1 - core) * OWN + s) * HALF, HALF), HALF), :] = swaps[s // PART][s % PART]
+        u_buf[pl.ds(pl.multiple_of((core * OWN + s) * HALF, HALF), HALF), :] = mine[s // PART][s % PART]
+        u_buf[pl.ds(pl.multiple_of(((1 - core) * OWN + s) * HALF, HALF), HALF), :] = theirs[s // PART][s % PART]
     copy.wait()
 
-    def q_part(j, carry):
+    def block(j, carry):
         c = pl.ds(pl.multiple_of(j * 256, 256), 256)
-        q[:, :, c] = dot_nt(u_buf[...], w_buf[c, :]).astype(BF16).reshape(2 * OWN, HALF, 256)
+        out[:, :, c] = dot_nt(u_buf[...], w_buf[c, :]).astype(BF16).reshape(2 * OWN, HALF, 256)
         return carry
 
-    lax.fori_loop(0, D // 256, q_part, 0)
-
-    def kv_part(j, carry):
-        c = pl.ds(pl.multiple_of(j * 256, 256), 256)
-        w = w_buf[pl.ds(pl.multiple_of(D + j * 256, 256), 256), :]
-        kv[:, :, c] = dot_nt(u_buf[...], w).astype(BF16).reshape(2 * OWN, HALF, 256)
-        return carry
-
-    lax.fori_loop(0, 2 * D // 256, kv_part, 0)
-
-
-def own_call(layer, keeps, swaps, w_tqkv):
+    lax.fori_loop(0, cols // 256, block, 0)
+
+
+def project_call(layer, mine, theirs, w_tqkv, start, cols):
     rows = 2 * OWN * HALF
     return pl.pallas_call(
-        functools.partial(own_kernel, layer=layer),
-        out_shape=[jax.ShapeDtypeStruct((2 * OWN, HALF, D), BF16), jax.ShapeDtypeStruct((2 * OWN, HALF, 2 * D), BF16)],
+        functools.partial(project_kernel, layer=layer, start=start, cols=cols),
+        out_shape=jax.ShapeDtypeStruct((2 * OWN, HALF, cols), BF16),
         in_specs=[VM] * (2 * OWN // PART) + [HB],
-        out_specs=[VM, VM],
-        scratch_shapes=[pltpu.VMEM((rows, D), BF16), pltpu.VMEM((3 * D, D), BF16), pltpu.SemaphoreType.DMA],
+        out_specs=VM,
+        scratch_shapes=[pltpu.VMEM((rows, D), BF16), pltpu.VMEM((cols, D), BF16), pltpu.SemaphoreType.DMA],
         compiler_params=pltpu.CompilerParams(vmem_limit_bytes=VMEM_LIMIT),
-        cost_estimate=pl.CostEstimate(flops=6 * rows * D * D, bytes_accessed=16 << 20, transcendentals=0),
-        name='temporal_own',
-    )(*keeps, *swaps, w_tqkv)
+        cost_estimate=pl.CostEstimate(flops=2 * rows * D * cols, bytes_accessed=8 << 20, transcendentals=0),
+        name='project',
+    )(*mine, *theirs, w_tqkv)
 
 
 def halo_kernel(*refs, layer):
     n = OWN // PART
-    q, kv_own = refs[:2]
-    near_k, near_s, up_k, up_s, down_k, down_s = (refs[2 + n * i:2 + n * i + n] for i in range(6))
-    bias_all, wqkv, o_keep, o_send, u_buf, kv, bias, w_buf, o_buf, sems, halo_sems = refs[2 + 6 * n:]
+    q, kv_near, kv_own = refs[:3]
+    up_k, up_s, down_k, down_s = (refs[3 + n * i:3 + n * i + n] for i in range(4))
+    bias_all, wqkv, o_keep, o_send, u_buf, kv, bias, w_buf, o_buf, sems, halo_sems = refs[3 + 4 * n:]
     pos = lax.axis_index('frames')
     core = lax.rem(pos, 2)
     other = 1 - core
@@ -281,11 +274,8 @@
     def into(src, slot, k):
         return [pltpu.make_async_copy(src[i], u_buf.at[pl.ds(slot + PART * i, PART)], halo_sems.at[k, i]) for i in range(n)]
 
-    near = into(near_k, core * OWN, 0) + into(near_s, other * OWN, 1)
-    up = into(up_k, (2 + core) * OWN, 2) + into(up_s, (2 + other) * OWN, 3)
-    down = into(down_k, (2 + core) * OWN, 2) + into(down_s, (2 + other) * OWN, 3)
-    for c in near:
-        c.start()
+    up = into(up_k, core * OWN, 0) + into(up_s, other * OWN, 1)
+    down = into(down_k, core * OWN, 0) + into(down_s, other * OWN, 1)
 
     @pl.when(row == 1)
     def _():
@@ -301,7 +291,9 @@
     c4.start()
     c5 = pltpu.make_async_copy(bias_all.at[layer], bias, sems.at[2])
     c5.start()
-    for c in [cw] + near + up:
+    c6 = pltpu.make_async_copy(kv_near, kv.at[pl.ds(0, 2 * OWN)], sems.at[3])
+    c6.start()
+    for c in [cw] + up:
         c.wait()
 
     def fill(i, carry):
@@ -309,12 +301,13 @@
         j = i % 8
         c = pl.ds(pl.multiple_of(j * 256, 256), 256)
         a = u_buf[pl.ds(s, 4)].reshape(4 * HALF, D)
-        kv[pl.ds(s, 4), :, c] = dot_nt(a, w_buf[c, :]).astype(BF16).reshape(4, HALF, 256)
+        kv[pl.ds(2 * OWN + s, 4), :, c] = dot_nt(a, w_buf[c, :]).astype(BF16).reshape(4, HALF, 256)
         return carry
 
-    lax.fori_loop(0, 32, fill, 0)
+    lax.fori_loop(0, 16, fill, 0)
     c4.wait()
     c5.wait()
+    c6.wait()
     low, high, is_low = half_masks()
 
     def attend(i, carry):
@@ -337,21 +330,21 @@
     o_send[...] = o_buf[pl.ds(other * OWN, OWN)]
 
 
-def halo_call(layer, q, kv_own, halos, bias, w_tqkv):
+def halo_call(layer, q, kv_near, kv_own, halos, bias, w_tqkv):
     n = 2 * OWN
     return pl.pallas_call(
         functools.partial(halo_kernel, layer=layer),
         out_shape=[jax.ShapeDtypeStruct((OWN, HALF, D), BF16)] * 2,
-        in_specs=[VM] + [HB] * (3 + len(halos)),
+        in_specs=[VM] + [HB] * (4 + len(halos)),
         out_specs=[VM, VM],
-        scratch_shapes=[pltpu.VMEM((2 * n, HALF, D), BF16), pltpu.VMEM((3 * n, HALF, 2 * D), BF16),
+        scratch_shapes=[pltpu.VMEM((n, HALF, D), BF16), pltpu.VMEM((3 * n, HALF, 2 * D), BF16),
                         pltpu.VMEM((16, 3 * n * GRP, n * GRP), F32), pltpu.VMEM((2 * D, D), BF16),
-                        pltpu.VMEM((n, HALF, D), BF16), pltpu.SemaphoreType.DMA((3,)),
-                        pltpu.SemaphoreType.DMA((4, OWN // PART))],
+                        pltpu.VMEM((n, HALF, D), BF16), pltpu.SemaphoreType.DMA((4,)),
+                        pltpu.SemaphoreType.DMA((2, OWN // PART))],
         compiler_params=pltpu.CompilerParams(vmem_limit_bytes=VMEM_LIMIT),
-        cost_estimate=pl.CostEstimate(flops=16 * n * HALF * D * D, bytes_accessed=16 << 20, transcendentals=0),
+        cost_estimate=pl.CostEstimate(flops=8 * n * HALF * D * D, bytes_accessed=16 << 20, transcendentals=0),
         name='temporal_halo',
-    )(q, kv_own, *halos, bias, w_tqkv)
+    )(q, kv_near, kv_own, *halos, bias, w_tqkv)
 
 
 def bias_kernel(lag, out):
@@ -395,6 +388,8 @@
     same = [(z * 4 + f, (z + 1) * 4 + f) for z in range(nz - 1) for f in range(4)]
     cross = [(z * 4 + f, (z + 1) * 4 + (f ^ 1)) for z in range(nz - 1) for f in range(4)]
 
+    back = [(i + 1, i) for i in range(4 * nz - 1)]
+
     def body(z_loc, mod_loc, step_loc, noise_loc, lag_bias, w_in, w_out, w_sqkv, w_so, w_tqkv, w_to, w_up, w_down):
         zc = lax.axis_index('tokens')
         fc = lax.axis_index('frames')
@@ -417,8 +412,8 @@
         mod = lax.dynamic_index_in_dim(mod, zc, 0, keepdims=False)
         mods = [[mod[p * PART:(p + 1) * PART, l] for p in range(OWN // PART)] for l in range(layers)]
 
-        def one_step(s, z_all):
-            z_cur = lax.dynamic_slice(z_all, (first, 0), (4, TOK * 4)).reshape(4 * TOK, 4)
+        def one_step(s, z_own):
+            z_cur = z_own.reshape(4 * TOK, 4)
             x = dot(z_cur.astype(BF16), w_in).astype(BF16).astype(F32)
             parts = range(OWN // PART)
             rows = PART * TOK
@@ -427,8 +422,13 @@
             for l in range(layers):
                 keeps, sends = [], []
                 for p in parts:
-                    ca = () if c_args is None else c_args + [mods[l - 1][p], to, w_up, w_down]
-                    xs[p], keep, send = dense_call(l - 1 if l else 0, p, l > 0, True, xs[p], ca, [mods[l][p], sq, so])
+                    a_args = [mods[l][p], sq, so]
+                    ca = () if l == 0 else c_args + [mods[l - 1][p], to, w_up, w_down]
+                    if l and p == OWN // PART - 1:
+                        xs[p] = dense_call(l - 1, p, True, False, xs[p], ca, ())[0]
+                        ca = ()
+                    fuse = bool(ca)
+                    xs[p], keep, send = dense_call(l - 1 if fuse else l, p, fuse, True, xs[p], ca, a_args)
                     keeps.append(keep)
                     sends.append(send)
 
@@ -445,9 +445,10 @@
                 swaps = move(sends, 'frames', [(0, 1), (1, 0), (2, 3), (3, 2)])
                 down_k = move(near_k, 'frames', [(2, 0), (3, 1)])
                 down_s = move(near_s, 'frames', [(2, 0), (3, 1)])
-                q, kv_own = own_call(l, keeps, swaps, tq)
-                halos = near_k + near_s + up_k + up_s + down_k + down_s
-                o_keep, o_send = halo_call(l, q, kv_own, halos, bias, tq)
+                q = project_call(l, keeps, swaps, tq, 0, D)
+                kv_own = project_call(l, keeps, swaps, tq, D, 2 * D)
+                kv_near = project_call(l, near_k, near_s, tq, D, 2 * D)
+                o_keep, o_send = halo_call(l, q, kv_near, kv_own, up_k + up_s + down_k + down_s, bias, tq)
                 o_recv = lax.ppermute(o_send, 'frames', [(0, 1), (1, 0), (2, 3), (3, 2)])
                 c_args = [o_keep, o_recv]
             xs = [dense_call(layers - 1, p, True, False, xs[p], c_args + [mods[layers - 1][p], to, w_up, w_down], ())[0]
@@ -455,16 +456,19 @@
             x = jnp.concatenate(xs, axis=0)
             vel = dot(norm_rows(x).astype(BF16), w_out)
             z_new = (z_cur + jnp.repeat(dt, TOK)[:, None] * vel).reshape(4, TOK * 4)
-            z_new = lax.all_gather(z_new, group, axis=0, tiled=True)
-            emit = lax.dynamic_slice(z_new[0].reshape(TOK, 4), (64 * zc + 16 * fc, 0), (16, 4))
-            return jnp.concatenate([z_new[1:], noise[s][None]], axis=0), emit
-
-        emits = []
+            after = lax.ppermute(z_new[0], group, back)
+            after = jnp.where(first == 16 * nz - 4, noise[s], after)
+            return jnp.concatenate([z_new[1:], after[None]], axis=0), z_new[:1]
+
+        z_own = lax.dynamic_slice(z_all, (first, 0), (4, TOK * 4))
+        heads = []
         for s in range(n_steps):
-            z_all, emit = one_step(s, z_all)
-            emits.append(emit)
-        z_out = lax.dynamic_slice(z_all.reshape(64, TOK, 4), (16 * fc, 64 * zc, 0), (16, 64, 4))
-        return jnp.stack(emits), z_out
+            z_own, head = one_step(s, z_own)
+            heads.append(head)
+        last = lax.all_gather(jnp.concatenate([z_own] + heads, axis=0), group, axis=0)
+        emits = lax.dynamic_slice(last[0, 4:].reshape(n_steps, TOK, 4), (0, 64 * zc + 16 * fc, 0), (n_steps, 16, 4))
+        z_out = lax.dynamic_slice(last[:, :4].reshape(16 * nz, TOK, 4), (16 * fc, 64 * zc, 0), (16, 64, 4))
+        return emits, z_out
 
     return jax.shard_map(body, mesh=mesh, in_specs=(slot_spec, mod_spec, step_spec, noise_spec) + (P(),) * 9,
                          out_specs=(emit_spec, slot_spec), check_vma=False)

time: 1470 us -> 1360 us (0.925)
  waiting for transfers between devices: 345 us -> 249 us
  Pallas kernels: 844 us -> 825 us
  blocking collectives: 70.8 us -> 53.5 us
    ppermute x84, waiting for transfers between devices: 331 us -> 232 us  [move(): out.append(lax.ppermute(vals[p], axes, pairs))]
    pallas_call x6 -> x18, Pallas kernels: 91.9 us -> 185 us  [project_call(): pl.pallas_call(functools.partial(project_kernel, layer=layer, start=start...]
    pallas_call x16 -> x20, Pallas kernels: 513 us -> 450 us  [dense_call(): pl.pallas_call(functools.partial(dense_kernel, do_c=do_c, do_a=do_a, ns=n...]
    pallas_call x6, Pallas kernels: 226 us -> 176 us  [halo_call(): pl.pallas_call(functools.partial(halo_kernel, layer=layer), out_shape=[ja...]
    all_gather x2 -> x1, blocking collectives: 38.5 us -> 21.3 us  [body(): lax.all_gather(jnp.concatenate([z_own] + heads, axis=0), group, axis=0)]
  transfers between devices with their start and end apart: 91 -> 93, of which waited for: 47 -> 38; matrix products, arithmetic and copies ran while one was open for 1% -> 1% of each run, Pallas kernels for 20% -> 29%
where the time goes in v2:
time: 1360 us; the launch traced here: 1340 us
  Pallas kernels  825 us (61%)
  waiting for transfers between devices  249 us (18%)
  starting transfers between devices  168 us (12%)
  blocking collectives  53.5 us (4%)
  local copies, waits for them, and re-layouts  36.7 us (3%)
    pallas_call x20, Pallas kernels, dense_call(): pl.pallas_call(functools.partial(dense_kernel, do_c=do_c, do_a=do_a, ns=n...  450 us
    ppermute x84, waiting for transfers between devices, move(): out.append(lax.ppermute(vals[p], axes, pairs))  232 us
    pallas_call x18, Pallas kernels, project_call(): pl.pallas_call(functools.partial(project_kernel, layer=layer, start=start...  185 us
    pallas_call x6, Pallas kernels, halo_call(): pl.pallas_call(functools.partial(halo_kernel, layer=layer), out_shape=[ja...  176 us
    ppermute x84, starting transfers between devices, move(): out.append(lax.ppermute(vals[p], axes, pairs))  160 us
    all_gather x1, blocking collectives, body(): lax.all_gather(small, group, axis=0).reshape(nz, 4, 17 + n_steps, 256)  32.3 us
  transfers between devices with their start and end apart: 93, of which 38 were waited for; matrix products, arithmetic and copies ran while one was open for 1% of the time, Pallas kernels for 29%

profile of v2, /device:TPU:0, one launch (start us, length us, event | category | flops | bytes accessed | tf_op | source)
XLA Modules:
  0.0 1343.5 jit_solution(12062814819423827935)
XLA Ops:
  8.2 32.3 %all-gather.2 = f32[16,19,256]{2,1,0:T(8,128)S(1)} all-gather(f32[1,19,256]{2,1,0:T(8,128)S(1)} %maximum_bitcast_fusion.1), channel_id=2, replica_groups=mesh['videos'=2,'tokens'=4,'frames'=4] {'tokens','frames'}, dimensions={0}, use_global_device_ids=true | all-gather | bytes 330752 | tf_op jit(solution)/shard_map/all_gather | solution.py:406
  74.7 18.3 %dense.21 = (f32[512,1024]{1,0:T(8,128)}, bf16[2,128,1024]{2,1,0:T(8,128)(2,1)}, bf16[2,128,1024]{2,1,0:T(8,128)(2,1)}) custom-call(f32[512,1024]{1,0:T(8,128)} %get-tuple-element.109.refs_0_, f32[2,6,1024]{2,1,0:T(8,128)} %get-tuple-element.114.refs_1_.refs_3_, bf16[3,3072,1024]{2,1,0:T(8,128)(2,1)} %bitcast.88, bf16[3,1024,1024]{2,1,0:T(8,128)(2,1)} %bitcast.112), custom_call_target="tpu_custom_call" | custom-call | flops 4294967296 | bytes 4194304 | tf_op jit(solution)/shard_map/dense/pallas_call | solution.py:216
  196.9 29.4 %temporal_halo.6 = (bf16[4,128,1024]{2,1,0:T(8,128)(2,1)}, bf16[4,128,1024]{2,1,0:T(8,128)(2,1)}) custom-call(bf16[8,128,1024]{2,1,0:T(8,128)(2,1)} %project.18.refs_0_, bf16[8,128,2048]{2,1,0:T(8,128)(2,1)} %project.19.refs_1_, bf16[8,128,2048]{2,1,0:T(8,128)(2,1)} %project.20.refs_2_, bf16[2,128,1024]{2,1,0:T(8,128)(2,1)} %collective-permute-done.6.refs_3_, ...), custom_call_target="tpu_custom_call" | custom-call | flops 8589934592 | bytes 16777216 | tf_op jit(solution)/shard_map/temporal_halo/pallas_call | solution.py:335
  229.4 34.3 %dense.22 = (f32[512,1024]{1,0:T(8,128)}, bf16[2,128,1024]{2,1,0:T(8,128)(2,1)}, bf16[2,128,1024]{2,1,0:T(8,128)(2,1)}) custom-call(f32[512,1024]{1,0:T(8,128)} %get-tuple-element.50.refs_0_, bf16[4,128,1024]{2,1,0:T(8,128)(2,1)} %get-tuple-element.55.refs_1_, bf16[4,128,1024]{2,1,0:T(8,128)(2,1)} %collective-permute-done.14.refs_2_, ...), custom_call_target="tpu_custom_call" | custom-call | flops 13958643712 | bytes 4194304 | tf_op jit(solution)/shard_map/dense/pallas_call | solution.py:216
  271.0 20.9 %dense.23.refs_0_ = f32[512,1024]{1,0:T(8,128)} custom-call(f32[512,1024]{1,0:T(8,128)} %get-tuple-element.59.refs_0_, bf16[4,128,1024]{2,1,0:T(8,128)(2,1)} %get-tuple-element.55.refs_1_, bf16[4,128,1024]{2,1,0:T(8,128)(2,1)} %collective-permute-done.14.refs_2_, f32[2,6,1024]{2,1,0:T(8,128)} %get-tuple-element.114.refs_1_.refs_3_, ...), custom_call_target="tpu_custom_call" | custom-call | flops 9663676416 | bytes 4194304 | tf_op jit(solution)/shard_map/dense/pallas_call | solution.py:216
  292.0 18.3 %dense.24 = (f32[512,1024]{1,0:T(8,128)}, bf16[2,128,1024]{2,1,0:T(8,128)(2,1)}, bf16[2,128,1024]{2,1,0:T(8,128)(2,1)}) custom-call(f32[512,1024]{1,0:T(8,128)} %dense.23.refs_0_, f32[2,6,1024]{2,1,0:T(8,128)} %get-tuple-element.112.refs_1_.refs_3_, bf16[3,3072,1024]{2,1,0:T(8,128)(2,1)} %bitcast.90, bf16[3,1024,1024]{2,1,0:T(8,128)(2,1)} %bitcast.114), custom_call_target="tpu_custom_call" | custom-call | flops 4294967296 | bytes 4194304 | tf_op jit(solution)/shard_map/dense/pallas_call | solution.py:216
  399.0 29.3 %temporal_halo.7 = (bf16[4,128,1024]{2,1,0:T(8,128)(2,1)}, bf16[4,128,1024]{2,1,0:T(8,128)(2,1)}) custom-call(bf16[8,128,1024]{2,1,0:T(8,128)(2,1)} %project.21.refs_0_, bf16[8,128,2048]{2,1,0:T(8,128)(2,1)} %project.22.refs_1_, bf16[8,128,2048]{2,1,0:T(8,128)(2,1)} %project.23.refs_2_, bf16[2,128,1024]{2,1,0:T(8,128)(2,1)} %collective-permute-done.21.refs_3_, ...), custom_call_target="tpu_custom_call" | custom-call | flops 8589934592 | bytes 16777216 | tf_op jit(solution)/shard_map/temporal_halo/pallas_call | solution.py:335
  431.4 34.3 %dense.25 = (f32[512,1024]{1,0:T(8,128)}, bf16[2,128,1024]{2,1,0:T(8,128)(2,1)}, bf16[2,128,1024]{2,1,0:T(8,128)(2,1)}) custom-call(f32[512,1024]{1,0:T(8,128)} %get-tuple-element.57.refs_0_, bf16[4,128,1024]{2,1,0:T(8,128)(2,1)} %get-tuple-element.63.refs_1_, bf16[4,128,1024]{2,1,0:T(8,128)(2,1)} %collective-permute-done.29.refs_2_, ...), custom_call_target="tpu_custom_call" | custom-call | flops 13958643712 | bytes 4194304 | tf_op jit(solution)/shard_map/dense/pallas_call | solution.py:216
  473.1 20.9 %dense.26.refs_0_ = f32[512,1024]{1,0:T(8,128)} custom-call(f32[512,1024]{1,0:T(8,128)} %get-tuple-element.67.refs_0_, bf16[4,128,1024]{2,1,0:T(8,128)(2,1)} %get-tuple-element.63.refs_1_, bf16[4,128,1024]{2,1,0:T(8,128)(2,1)} %collective-permute-done.29.refs_2_, f32[2,6,1024]{2,1,0:T(8,128)} %get-tuple-element.112.refs_1_.refs_3_, ...), custom_call_target="tpu_custom_call" | custom-call | flops 9663676416 | bytes 4194304 | tf_op jit(solution)/shard_map/dense/pallas_call | solution.py:216
  601.1 29.3 %temporal_halo.8 = (bf16[4,128,1024]{2,1,0:T(8,128)(2,1)}, bf16[4,128,1024]{2,1,0:T(8,128)(2,1)}) custom-call(bf16[8,128,1024]{2,1,0:T(8,128)(2,1)} %project.24.refs_0_, bf16[8,128,2048]{2,1,0:T(8,128)(2,1)} %project.25.refs_1_, bf16[8,128,2048]{2,1,0:T(8,128)(2,1)} %project.26.refs_2_, bf16[2,128,1024]{2,1,0:T(8,128)(2,1)} %collective-permute-done.36.refs_3_, ...), custom_call_target="tpu_custom_call" | custom-call | flops 8589934592 | bytes 16777216 | tf_op jit(solution)/shard_map/temporal_halo/pallas_call | solution.py:335
  633.5 20.9 %dense.29 = f32[512,1024]{1,0:T(8,128)} custom-call(f32[512,1024]{1,0:T(8,128)} %get-tuple-element.73.refs_0_, bf16[4,128,1024]{2,1,0:T(8,128)(2,1)} %get-tuple-element.71.refs_1_, bf16[4,128,1024]{2,1,0:T(8,128)(2,1)} %collective-permute-done.44.refs_2_, f32[2,6,1024]{2,1,0:T(8,128)} %get-tuple-element.111.refs_1_.refs_3_, ...), custom_call_target="tpu_custom_call" | custom-call | flops 9663676416 | bytes 4194304 | tf_op jit(solution)/shard_map/dense/pallas_call | solution.py:216
  654.4 20.8 %dense.28 = f32[512,1024]{1,0:T(8,128)} custom-call(f32[512,1024]{1,0:T(8,128)} %get-tuple-element.65.refs_0_, bf16[4,128,1024]{2,1,0:T(8,128)(2,1)} %get-tuple-element.71.refs_1_, bf16[4,128,1024]{2,1,0:T(8,128)(2,1)} %collective-permute-done.44.refs_2_, f32[2,6,1024]{2,1,0:T(8,128)} %get-tuple-element.110.refs_7_.refs_3_, ...), custom_call_target="tpu_custom_call" | custom-call | flops 9663676416 | bytes 4194304 | tf_op jit(solution)/shard_map/dense/pallas_call | solution.py:216
  714.5 18.3 %dense.31 = (f32[512,1024]{1,0:T(8,128)}, bf16[2,128,1024]{2,1,0:T(8,128)(2,1)}, bf16[2,128,1024]{2,1,0:T(8,128)(2,1)}) custom-call(f32[512,1024]{1,0:T(8,128)} %get-tuple-element.107.refs_0_, f32[2,6,1024]{2,1,0:T(8,128)} %get-tuple-element.114.refs_1_.refs_3_, bf16[3,3072,1024]{2,1,0:T(8,128)(2,1)} %bitcast.94, bf16[3,1024,1024]{2,1,0:T(8,128)(2,1)} %bitcast.118), custom_call_target="tpu_custom_call" | custom-call | flops 4294967296 | bytes 4194304 | tf_op jit(solution)/shard_map/dense/pallas_call | solution.py:216
  822.1 29.4 %temporal_halo.9 = (bf16[4,128,1024]{2,1,0:T(8,128)(2,1)}, bf16[4,128,1024]{2,1,0:T(8,128)(2,1)}) custom-call(bf16[8,128,1024]{2,1,0:T(8,128)(2,1)} %project.27.refs_0_, bf16[8,128,2048]{2,1,0:T(8,128)(2,1)} %project.28.refs_1_, bf16[8,128,2048]{2,1,0:T(8,128)(2,1)} %project.29.refs_2_, bf16[2,128,1024]{2,1,0:T(8,128)(2,1)} %collective-permute-done.52.refs_3_, ...), custom_call_target="tpu_custom_call" | custom-call | flops 8589934592 | bytes 16777216 | tf_op jit(solution)/shard_map/temporal_halo/pallas_call | solution.py:335
  854.6 34.3 %dense.32 = (f32[512,1024]{1,0:T(8,128)}, bf16[2,128,1024]{2,1,0:T(8,128)(2,1)}, bf16[2,128,1024]{2,1,0:T(8,128)(2,1)}) custom-call(f32[512,1024]{1,0:T(8,128)} %get-tuple-element.74.refs_0_, bf16[4,128,1024]{2,1,0:T(8,128)(2,1)} %get-tuple-element.79.refs_1_, bf16[4,128,1024]{2,1,0:T(8,128)(2,1)} %collective-permute-done.60.refs_2_, ...), custom_call_target="tpu_custom_call" | custom-call | flops 13958643712 | bytes 4194304 | tf_op jit(solution)/shard_map/dense/pallas_call | solution.py:216
  896.4 20.9 %dense.33.refs_0_ = f32[512,1024]{1,0:T(8,128)} custom-call(f32[512,1024]{1,0:T(8,128)} %get-tuple-element.83.refs_0_, bf16[4,128,1024]{2,1,0:T(8,128)(2,1)} %get-tuple-element.79.refs_1_, bf16[4,128,1024]{2,1,0:T(8,128)(2,1)} %collective-permute-done.60.refs_2_, f32[2,6,1024]{2,1,0:T(8,128)} %get-tuple-element.114.refs_1_.refs_3_, ...), custom_call_target="tpu_custom_call" | custom-call | flops 9663676416 | bytes 4194304 | tf_op jit(solution)/shard_map/dense/pallas_call | solution.py:216
  917.3 18.3 %dense.34 = (f32[512,1024]{1,0:T(8,128)}, bf16[2,128,1024]{2,1,0:T(8,128)(2,1)}, bf16[2,128,1024]{2,1,0:T(8,128)(2,1)}) custom-call(f32[512,1024]{1,0:T(8,128)} %dense.33.refs_0_, f32[2,6,1024]{2,1,0:T(8,128)} %get-tuple-element.112.refs_1_.refs_3_, bf16[3,3072,1024]{2,1,0:T(8,128)(2,1)} %bitcast.96, bf16[3,1024,1024]{2,1,0:T(8,128)(2,1)} %bitcast.120), custom_call_target="tpu_custom_call" | custom-call | flops 4294967296 | bytes 4194304 | tf_op jit(solution)/shard_map/dense/pallas_call | solution.py:216
  1024.3 29.3 %temporal_halo.10 = (bf16[4,128,1024]{2,1,0:T(8,128)(2,1)}, bf16[4,128,1024]{2,1,0:T(8,128)(2,1)}) custom-call(bf16[8,128,1024]{2,1,0:T(8,128)(2,1)} %project.30.refs_0_, bf16[8,128,2048]{2,1,0:T(8,128)(2,1)} %project.31.refs_1_, bf16[8,128,2048]{2,1,0:T(8,128)(2,1)} %project.32.refs_2_, bf16[2,128,1024]{2,1,0:T(8,128)(2,1)} %collective-permute-done.67.refs_3_, ...), custom_call_target="tpu_custom_call" | custom-call | flops 8589934592 | bytes 16777216 | tf_op jit(solution)/shard_map/temporal_halo/pallas_call | solution.py:335
  1056.7 34.4 %dense.35 = (f32[512,1024]{1,0:T(8,128)}, bf16[2,128,1024]{2,1,0:T(8,128)(2,1)}, bf16[2,128,1024]{2,1,0:T(8,128)(2,1)}) custom-call(f32[512,1024]{1,0:T(8,128)} %get-tuple-element.81.refs_0_, bf16[4,128,1024]{2,1,0:T(8,128)(2,1)} %get-tuple-element.87.refs_1_, bf16[4,128,1024]{2,1,0:T(8,128)(2,1)} %collective-permute-done.75.refs_2_, ...), custom_call_target="tpu_custom_call" | custom-call | flops 13958643712 | bytes 4194304 | tf_op jit(solution)/shard_map/dense/pallas_call | solution.py:216
  1098.4 20.9 %dense.36.refs_0_ = f32[512,1024]{1,0:T(8,128)} custom-call(f32[512,1024]{1,0:T(8,128)} %get-tuple-element.91.refs_0_, bf16[4,128,1024]{2,1,0:T(8,128)(2,1)} %get-tuple-element.87.refs_1_, bf16[4,128,1024]{2,1,0:T(8,128)(2,1)} %collective-permute-done.75.refs_2_, f32[2,6,1024]{2,1,0:T(8,128)} %get-tuple-element.112.refs_1_.refs_3_, ...), custom_call_target="tpu_custom_call" | custom-call | flops 9663676416 | bytes 4194304 | tf_op jit(solution)/shard_map/dense/pallas_call | solution.py:216
  1226.3 29.3 %temporal_halo.11 = (bf16[4,128,1024]{2,1,0:T(8,128)(2,1)}, bf16[4,128,1024]{2,1,0:T(8,128)(2,1)}) custom-call(bf16[8,128,1024]{2,1,0:T(8,128)(2,1)} %project.33.refs_0_, bf16[8,128,2048]{2,1,0:T(8,128)(2,1)} %project.34.refs_1_, bf16[8,128,2048]{2,1,0:T(8,128)(2,1)} %project.35.refs_2_, bf16[2,128,1024]{2,1,0:T(8,128)(2,1)} %collective-permute-done.82.refs_3_, ...), custom_call_target="tpu_custom_call" | custom-call | flops 8589934592 | bytes 16777216 | tf_op jit(solution)/shard_map/temporal_halo/pallas_call | solution.py:335
  1258.8 20.8 %dense.39 = f32[512,1024]{1,0:T(8,128)} custom-call(f32[512,1024]{1,0:T(8,128)} %get-tuple-element.97.refs_0_, bf16[4,128,1024]{2,1,0:T(8,128)(2,1)} %get-tuple-element.95.refs_1_, bf16[4,128,1024]{2,1,0:T(8,128)(2,1)} %collective-permute-done.90.refs_2_, f32[2,6,1024]{2,1,0:T(8,128)} %get-tuple-element.111.refs_1_.refs_3_, ...), custom_call_target="tpu_custom_call" | custom-call | flops 9663676416 | bytes 4194304 | tf_op jit(solution)/shard_map/dense/pallas_call | solution.py:216
  1279.6 20.8 %dense.38 = f32[512,1024]{1,0:T(8,128)} custom-call(f32[512,1024]{1,0:T(8,128)} %get-tuple-element.89.refs_0_, bf16[4,128,1024]{2,1,0:T(8,128)(2,1)} %get-tuple-element.95.refs_1_, bf16[4,128,1024]{2,1,0:T(8,128)(2,1)} %collective-permute-done.90.refs_2_, f32[2,6,1024]{2,1,0:T(8,128)} %get-tuple-element.110.refs_7_.refs_3_, ...), custom_call_target="tpu_custom_call" | custom-call | flops 9663676416 | bytes 4194304 | tf_op jit(solution)/shard_map/dense/pallas_call | solution.py:216
  1308.9 21.3 %all-gather.3 = f32[16,6,1024]{2,1,0:T(8,128)S(1)} all-gather(f32[1,6,1024]{2,1,0:T(8,128)S(1)} %maximum_bitcast_fusion), channel_id=3, replica_groups=mesh['videos'=2,'tokens'=4,'frames'=4] {'tokens','frames'}, dimensions={0}, use_global_device_ids=true | all-gather | bytes 417792 | tf_op jit(solution)/shard_map/all_gather | solution.py:468
  (342 shorter events, 734.0 us)
Async XLA Ops:
  3.5 46.9 %all-to-all-start = ((f32[4,4,3,6,1024]{4,1,3,2,0:T(4,128)}), f32[4,4,3,6,1024]{4,1,3,2,0:T(4,128)}, u32[]{:S(2)}, u32[]{:S(2)}) async-start(f32[4,4,3,6,1024]{4,1,3,2,0:T(4,128)} %copy.78), calls=%async_computation | async-start | bytes 2359296 | tf_op jit(solution)/shard_map/all_to_all | solution.py:411
  97.3 45.4 %collective-permute-start.8 = (bf16[2,128,1024]{2,1,0:T(8,128)(2,1)}, bf16[2,128,1024]{2,1,0:T(8,128)(2,1)}, u32[]{:S(2)}, u32[]{:S(2)}) collective-permute-start(bf16[2,128,1024]{2,1,0:T(8,128)(2,1)} %get-tuple-element.53), channel_id=1, source_target_pairs={{0,3},{1,2},{4,7},{5,6},{8,11},{9,10},{12,15},{13,14},{16,19},{17,... | collective-permute-start | bytes 1572872 | tf_op jit(solution)/shard_map/ppermute | solution.py:438
  101.4 45.6 %collective-permute-start = (bf16[2,128,1024]{2,1,0:T(8,128)(2,1)}, bf16[2,128,1024]{2,1,0:T(8,128)(2,1)}, u32[]{:S(2)}, u32[]{:S(2)}) collective-permute-start(bf16[2,128,1024]{2,1,0:T(8,128)(2,1)} %get-tuple-element.53), channel_id=1, source_target_pairs={{0,1},{1,0},{2,3},{3,2},{4,5},{5,4},{6,7},{7,6},{8,9},{9,8},{10,11... | collective-permute-start | bytes 1572872 | tf_op jit(solution)/shard_map/ppermute | solution.py:438
  101.6 46.6 %collective-permute-start.6 = (bf16[2,128,1024]{2,1,0:T(8,128)(2,1)S(1)}, bf16[2,128,1024]{2,1,0:T(8,128)(2,1)}, u32[]{:S(2)}, u32[]{:S(2)}) collective-permute-start(bf16[2,128,1024]{2,1,0:T(8,128)(2,1)S(1)} %copy-done.14), channel_id=1, source_target_pairs={{0,2},{1,3},{4,6},{5,7},{8,10},{9,11},{12,14},{13,15},{16,18},{17,... | collective-permute-start | bytes 1572872 | tf_op jit(solution)/shard_map/ppermute | solution.py:438
  106.9 42.6 %collective-permute-start.9 = (bf16[2,128,1024]{2,1,0:T(8,128)(2,1)}, bf16[2,128,1024]{2,1,0:T(8,128)(2,1)}, u32[]{:S(2)}, u32[]{:S(2)}) collective-permute-start(bf16[2,128,1024]{2,1,0:T(8,128)(2,1)} %get-tuple-element.54), channel_id=1, source_target_pairs={{0,3},{1,2},{4,7},{5,6},{8,11},{9,10},{12,15},{13,14},{16,19},{17,... | collective-permute-start | bytes 1572872 | tf_op jit(solution)/shard_map/ppermute | solution.py:438
  149.5 36.9 %collective-permute-start.13 = (bf16[2,128,1024]{2,1,0:T(8,128)(2,1)}, bf16[2,128,1024]{2,1,0:T(8,128)(2,1)}, u32[]{:S(2)}, u32[]{:S(2)}) collective-permute-start(bf16[2,128,1024]{2,1,0:T(8,128)(2,1)} %collective-permute-done.5.refs_3_), channel_id=1, source_target_pairs={{2,0},{3,1},{6,4},{7,5},{10,8},{11,9},{14,12},{15,13},{18,16},{19,... | collective-permute-start | bytes 1572872 | tf_op jit(solution)/shard_map/ppermute | solution.py:438
  150.9 46.0 %collective-permute-start.11 = (bf16[2,128,1024]{2,1,0:T(8,128)(2,1)}, bf16[2,128,1024]{2,1,0:T(8,128)(2,1)}, u32[]{:S(2)}, u32[]{:S(2)}) collective-permute-start(bf16[2,128,1024]{2,1,0:T(8,128)(2,1)} %collective-permute-done.3.refs_1_), channel_id=1, source_target_pairs={{2,0},{3,1},{6,4},{7,5},{10,8},{11,9},{14,12},{15,13},{18,16},{19,... | collective-permute-start | bytes 1572872 | tf_op jit(solution)/shard_map/ppermute | solution.py:438
  263.7 52.8 %collective-permute-start.19 = (bf16[2,128,1024]{2,1,0:T(8,128)(2,1)}, bf16[2,128,1024]{2,1,0:T(8,128)(2,1)}, u32[]{:S(2)}, u32[]{:S(2)}) collective-permute-start(bf16[2,128,1024]{2,1,0:T(8,128)(2,1)} %get-tuple-element.61), channel_id=1, source_target_pairs={{0,5},{1,4},{2,7},{3,6},{4,9},{5,8},{6,11},{7,10},{8,13},{9,12},{1... | collective-permute-start | bytes 1572872 | tf_op jit(solution)/shard_map/ppermute | solution.py:438
  268.7 48.1 %collective-permute-start.17 = (bf16[2,128,1024]{2,1,0:T(8,128)(2,1)}, bf16[2,128,1024]{2,1,0:T(8,128)(2,1)}, u32[]{:S(2)}, u32[]{:S(2)}) collective-permute-start(bf16[2,128,1024]{2,1,0:T(8,128)(2,1)} %get-tuple-element.58.refs_0_), channel_id=1, source_target_pairs={{0,4},{1,5},{2,6},{3,7},{4,8},{5,9},{6,10},{7,11},{8,12},{9,13},{1... | collective-permute-start | bytes 1572872 | tf_op jit(solution)/shard_map/ppermute | solution.py:438
  352.7 46.3 %collective-permute-start.26 = (bf16[2,128,1024]{2,1,0:T(8,128)(2,1)}, bf16[2,128,1024]{2,1,0:T(8,128)(2,1)}, u32[]{:S(2)}, u32[]{:S(2)}) collective-permute-start(bf16[2,128,1024]{2,1,0:T(8,128)(2,1)} %collective-permute-done.18.refs_1_), channel_id=1, source_target_pairs={{2,0},{3,1},{6,4},{7,5},{10,8},{11,9},{14,12},{15,13},{18,16},{19,... | collective-permute-start | bytes 1572872 | tf_op jit(solution)/shard_map/ppermute | solution.py:438
  465.7 52.9 %collective-permute-start.34 = (bf16[2,128,1024]{2,1,0:T(8,128)(2,1)}, bf16[2,128,1024]{2,1,0:T(8,128)(2,1)}, u32[]{:S(2)}, u32[]{:S(2)}) collective-permute-start(bf16[2,128,1024]{2,1,0:T(8,128)(2,1)} %get-tuple-element.69), channel_id=1, source_target_pairs={{0,5},{1,4},{2,7},{3,6},{4,9},{5,8},{6,11},{7,10},{8,13},{9,12},{1... | collective-permute-start | bytes 1572872 | tf_op jit(solution)/shard_map/ppermute | solution.py:438
  470.6 48.2 %collective-permute-start.32 = (bf16[2,128,1024]{2,1,0:T(8,128)(2,1)}, bf16[2,128,1024]{2,1,0:T(8,128)(2,1)}, u32[]{:S(2)}, u32[]{:S(2)}) collective-permute-start(bf16[2,128,1024]{2,1,0:T(8,128)(2,1)} %get-tuple-element.66.refs_0_), channel_id=1, source_target_pairs={{0,4},{1,5},{2,6},{3,7},{4,8},{5,9},{6,10},{7,11},{8,12},{9,13},{1... | collective-permute-start | bytes 1572872 | tf_op jit(solution)/shard_map/ppermute | solution.py:438
  553.6 36.9 %collective-permute-start.43 = (bf16[2,128,1024]{2,1,0:T(8,128)(2,1)}, bf16[2,128,1024]{2,1,0:T(8,128)(2,1)}, u32[]{:S(2)}, u32[]{:S(2)}) collective-permute-start(bf16[2,128,1024]{2,1,0:T(8,128)(2,1)} %collective-permute-done.35.refs_3_), channel_id=1, source_target_pairs={{2,0},{3,1},{6,4},{7,5},{10,8},{11,9},{14,12},{15,13},{18,16},{19,... | collective-permute-start | bytes 1572872 | tf_op jit(solution)/shard_map/ppermute | solution.py:438
  554.9 46.2 %collective-permute-start.41 = (bf16[2,128,1024]{2,1,0:T(8,128)(2,1)}, bf16[2,128,1024]{2,1,0:T(8,128)(2,1)}, u32[]{:S(2)}, u32[]{:S(2)}) collective-permute-start(bf16[2,128,1024]{2,1,0:T(8,128)(2,1)} %collective-permute-done.33.refs_1_), channel_id=1, source_target_pairs={{2,0},{3,1},{6,4},{7,5},{10,8},{11,9},{14,12},{15,13},{18,16},{19,... | collective-permute-start | bytes 1572872 | tf_op jit(solution)/shard_map/ppermute | solution.py:438
  774.7 36.9 %collective-permute-start.59 = (bf16[2,128,1024]{2,1,0:T(8,128)(2,1)}, bf16[2,128,1024]{2,1,0:T(8,128)(2,1)}, u32[]{:S(2)}, u32[]{:S(2)}) collective-permute-start(bf16[2,128,1024]{2,1,0:T(8,128)(2,1)} %collective-permute-done.51.refs_3_), channel_id=1, source_target_pairs={{2,0},{3,1},{6,4},{7,5},{10,8},{11,9},{14,12},{15,13},{18,16},{19,... | collective-permute-start | bytes 1572872 | tf_op jit(solution)/shard_map/ppermute | solution.py:438
  776.0 46.0 %collective-permute-start.57 = (bf16[2,128,1024]{2,1,0:T(8,128)(2,1)}, bf16[2,128,1024]{2,1,0:T(8,128)(2,1)}, u32[]{:S(2)}, u32[]{:S(2)}) collective-permute-start(bf16[2,128,1024]{2,1,0:T(8,128)(2,1)} %collective-permute-done.49.refs_1_), channel_id=1, source_target_pairs={{2,0},{3,1},{6,4},{7,5},{10,8},{11,9},{14,12},{15,13},{18,16},{19,... | collective-permute-start | bytes 1572872 | tf_op jit(solution)/shard_map/ppermute | solution.py:438
  888.9 53.0 %collective-permute-start.65 = (bf16[2,128,1024]{2,1,0:T(8,128)(2,1)}, bf16[2,128,1024]{2,1,0:T(8,128)(2,1)}, u32[]{:S(2)}, u32[]{:S(2)}) collective-permute-start(bf16[2,128,1024]{2,1,0:T(8,128)(2,1)} %get-tuple-element.85), channel_id=1, source_target_pairs={{0,5},{1,4},{2,7},{3,6},{4,9},{5,8},{6,11},{7,10},{8,13},{9,12},{1... | collective-permute-start | bytes 1572872 | tf_op jit(solution)/shard_map/ppermute | solution.py:438
  893.9 48.2 %collective-permute-start.63 = (bf16[2,128,1024]{2,1,0:T(8,128)(2,1)}, bf16[2,128,1024]{2,1,0:T(8,128)(2,1)}, u32[]{:S(2)}, u32[]{:S(2)}) collective-permute-start(bf16[2,128,1024]{2,1,0:T(8,128)(2,1)} %get-tuple-element.82.refs_0_), channel_id=1, source_target_pairs={{0,4},{1,5},{2,6},{3,7},{4,8},{5,9},{6,10},{7,11},{8,12},{9,13},{1... | collective-permute-start | bytes 1572872 | tf_op jit(solution)/shard_map/ppermute | solution.py:438
  976.7 36.9 %collective-permute-start.74 = (bf16[2,128,1024]{2,1,0:T(8,128)(2,1)}, bf16[2,128,1024]{2,1,0:T(8,128)(2,1)}, u32[]{:S(2)}, u32[]{:S(2)}) collective-permute-start(bf16[2,128,1024]{2,1,0:T(8,128)(2,1)} %collective-permute-done.66.refs_3_), channel_id=1, source_target_pairs={{2,0},{3,1},{6,4},{7,5},{10,8},{11,9},{14,12},{15,13},{18,16},{19,... | collective-permute-start | bytes 1572872 | tf_op jit(solution)/shard_map/ppermute | solution.py:438
  978.1 46.3 %collective-permute-start.72 = (bf16[2,128,1024]{2,1,0:T(8,128)(2,1)}, bf16[2,128,1024]{2,1,0:T(8,128)(2,1)}, u32[]{:S(2)}, u32[]{:S(2)}) collective-permute-start(bf16[2,128,1024]{2,1,0:T(8,128)(2,1)} %collective-permute-done.64.refs_1_), channel_id=1, source_target_pairs={{2,0},{3,1},{6,4},{7,5},{10,8},{11,9},{14,12},{15,13},{18,16},{19,... | collective-permute-start | bytes 1572872 | tf_op jit(solution)/shard_map/ppermute | solution.py:438
  1091.1 52.8 %collective-permute-start.80 = (bf16[2,128,1024]{2,1,0:T(8,128)(2,1)}, bf16[2,128,1024]{2,1,0:T(8,128)(2,1)}, u32[]{:S(2)}, u32[]{:S(2)}) collective-permute-start(bf16[2,128,1024]{2,1,0:T(8,128)(2,1)} %get-tuple-element.93), channel_id=1, source_target_pairs={{0,5},{1,4},{2,7},{3,6},{4,9},{5,8},{6,11},{7,10},{8,13},{9,12},{1... | collective-permute-start | bytes 1572872 | tf_op jit(solution)/shard_map/ppermute | solution.py:438
  1096.0 48.1 %collective-permute-start.78 = (bf16[2,128,1024]{2,1,0:T(8,128)(2,1)}, bf16[2,128,1024]{2,1,0:T(8,128)(2,1)}, u32[]{:S(2)}, u32[]{:S(2)}) collective-permute-start(bf16[2,128,1024]{2,1,0:T(8,128)(2,1)} %get-tuple-element.90.refs_0_), channel_id=1, source_target_pairs={{0,4},{1,5},{2,6},{3,7},{4,8},{5,9},{6,10},{7,11},{8,12},{9,13},{1... | collective-permute-start | bytes 1572872 | tf_op jit(solution)/shard_map/ppermute | solution.py:438
  1178.9 36.9 %collective-permute-start.89 = (bf16[2,128,1024]{2,1,0:T(8,128)(2,1)}, bf16[2,128,1024]{2,1,0:T(8,128)(2,1)}, u32[]{:S(2)}, u32[]{:S(2)}) collective-permute-start(bf16[2,128,1024]{2,1,0:T(8,128)(2,1)} %collective-permute-done.81.refs_3_), channel_id=1, source_target_pairs={{2,0},{3,1},{6,4},{7,5},{10,8},{11,9},{14,12},{15,13},{18,16},{19,... | collective-permute-start | bytes 1572872 | tf_op jit(solution)/shard_map/ppermute | solution.py:438
  1180.2 46.2 %collective-permute-start.87 = (bf16[2,128,1024]{2,1,0:T(8,128)(2,1)}, bf16[2,128,1024]{2,1,0:T(8,128)(2,1)}, u32[]{:S(2)}, u32[]{:S(2)}) collective-permute-start(bf16[2,128,1024]{2,1,0:T(8,128)(2,1)} %collective-permute-done.79.refs_1_), channel_id=1, source_target_pairs={{2,0},{3,1},{6,4},{7,5},{10,8},{11,9},{14,12},{15,13},{18,16},{19,... | collective-permute-start | bytes 1572872 | tf_op jit(solution)/shard_map/ppermute | solution.py:438
  (100 other events, 2123.8 us)

commit v3 on v2

--- a/solution.py
+++ b/solution.py
@@ -21,6 +21,7 @@
 NT = (((1,), (1,)), ((), ()))
 TN = (((0,), (0,)), ((), ()))
 PART = 2
+COLS = 512
 
 
 def dot(a, b):
@@ -119,11 +120,11 @@
         arrive(0)
 
         def proj(j, carry):
-            c = pl.ds(pl.multiple_of(j * 256, 256), 256)
+            c = pl.ds(pl.multiple_of(j * COLS, COLS), COLS)
             x[:, c] = x_in[:, c] + dot(o_buf[...], vto[:, c])
             return carry
 
-        lax.fori_loop(0, D // 256, proj, 0)
+        lax.fori_loop(0, D // COLS, proj, 0)
         for s in range(ns):
             norm_mod(x, s * TOK, u_buf, s * TOK, mod_c[s, 4:5, :], mod_c[s, 5:6, :], TOK)
         arrive(1)
@@ -132,20 +133,20 @@
             rb = pl.ds(b * hrows, hrows)
 
             def up(j, carry):
-                c = pl.ds(pl.multiple_of(j * 256, 256), 256)
+                c = pl.ds(pl.multiple_of(j * COLS, COLS), COLS)
                 h_buf[:, c] = gelu(dot(u_buf[rb, :], vup[:, c])).astype(BF16)
                 return carry
 
-            lax.fori_loop(0, HID // 256, up, 0)
+            lax.fori_loop(0, HID // COLS, up, 0)
             if b == 0:
                 arrive(2)
 
             def down(j, carry):
-                c = pl.ds(pl.multiple_of(j * 256, 256), 256)
+                c = pl.ds(pl.multiple_of(j * COLS, COLS), COLS)
                 x[rb, c] = x[rb, c] + dot(h_buf[...], vdn[:, c])
                 return carry
 
-            lax.fori_loop(0, D // 256, down, 0)
+            lax.fori_loop(0, D // COLS, down, 0)
         k = 3
     else:
         x[...] = x_in[...]
@@ -155,11 +156,11 @@
         arrive(k)
 
         def qkv(j, carry):
-            c = pl.ds(pl.multiple_of(j * 256, 256), 256)
+            c = pl.ds(pl.multiple_of(j * COLS, COLS), COLS)
             qkv_buf[:, c] = dot_nt(u_buf[...], vsqkv[c, :]).astype(BF16)
             return carry
 
-        lax.fori_loop(0, 3 * D // 256, qkv, 0)
+        lax.fori_loop(0, 3 * D // COLS, qkv, 0)
         low, high, is_low = half_masks()
 
         def attend(i, carry):
@@ -178,11 +179,11 @@
         arrive(k + 1)
 
         def proj_s(j, carry):
-            c = pl.ds(pl.multiple_of(j * 256, 256), 256)
+            c = pl.ds(pl.multiple_of(j * COLS, COLS), COLS)
             x[:, c] = x[:, c] + dot(o_buf[...], vso[:, c])
             return carry
 
-        lax.fori_loop(0, D // 256, proj_s, 0)
+        lax.fori_loop(0, D // COLS, proj_s, 0)
         for s in range(ns):
             norm_mod(x, s * TOK + core * HALF, u_keep.at[s], 0, mod_a[s, 2:3, :], mod_a[s, 3:4, :], HALF)
             norm_mod(x, s * TOK + (1 - core) * HALF, u_send.at[s], 0, mod_a[s, 2:3, :], mod_a[s, 3:4, :], HALF)
@@ -225,34 +226,31 @@
     )(*args)
 
 
-def project_kernel(*refs, layer, start, cols):
+def project_kernel(*refs):
     n = OWN // PART
     mine, theirs = refs[:n], refs[n:2 * n]
-    wqkv, out, u_buf, w_buf, sem = refs[2 * n:]
+    w_blk, out, u_buf = refs[2 * n:]
     core = lax.rem(lax.axis_index('frames'), 2)
-    copy = pltpu.make_async_copy(wqkv.at[layer, pl.ds(start, cols)], w_buf, sem)
-    copy.start()
-    for s in range(OWN):
-        u_buf[pl.ds(pl.multiple_of((core * OWN + s) * HALF, HALF), HALF), :] = mine[s // PART][s % PART]
-        u_buf[pl.ds(pl.multiple_of(((1 - core) * OWN + s) * HALF, HALF), HALF), :] = theirs[s // PART][s % PART]
-    copy.wait()
-
-    def block(j, carry):
-        c = pl.ds(pl.multiple_of(j * 256, 256), 256)
-        out[:, :, c] = dot_nt(u_buf[...], w_buf[c, :]).astype(BF16).reshape(2 * OWN, HALF, 256)
-        return carry
-
-    lax.fori_loop(0, cols // 256, block, 0)
-
-
-def project_call(layer, mine, theirs, w_tqkv, start, cols):
+
+    @pl.when(pl.program_id(0) == 0)
+    def _():
+        for s in range(OWN):
+            u_buf[pl.ds(pl.multiple_of((core * OWN + s) * HALF, HALF), HALF), :] = mine[s // PART][s % PART]
+            u_buf[pl.ds(pl.multiple_of(((1 - core) * OWN + s) * HALF, HALF), HALF), :] = theirs[s // PART][s % PART]
+
+    out[...] = dot_nt(u_buf[...], w_blk[...]).astype(BF16).reshape(2 * OWN, HALF, out.shape[-1])
+
+
+def project_call(layer, mine, theirs, w_tqkv, start, cols, blk=512):
     rows = 2 * OWN * HALF
     return pl.pallas_call(
-        functools.partial(project_kernel, layer=layer, start=start, cols=cols),
+        project_kernel,
+        grid=(cols // blk,),
         out_shape=jax.ShapeDtypeStruct((2 * OWN, HALF, cols), BF16),
-        in_specs=[VM] * (2 * OWN // PART) + [HB],
-        out_specs=VM,
-        scratch_shapes=[pltpu.VMEM((rows, D), BF16), pltpu.VMEM((cols, D), BF16), pltpu.SemaphoreType.DMA],
+        in_specs=[pl.BlockSpec((PART, HALF, D), lambda j: (0, 0, 0))] * (2 * OWN // PART)
+        + [pl.BlockSpec((None, blk, D), lambda j: (layer, start // blk + j, 0))],
+        out_specs=pl.BlockSpec((2 * OWN, HALF, blk), lambda j: (0, 0, j)),
+        scratch_shapes=[pltpu.VMEM((rows, D), BF16)],
         compiler_params=pltpu.CompilerParams(vmem_limit_bytes=VMEM_LIMIT),
         cost_estimate=pl.CostEstimate(flops=2 * rows * D * cols, bytes_accessed=8 << 20, transcendentals=0),
         name='project',
@@ -297,14 +295,14 @@
         c.wait()
 
     def fill(i, carry):
-        s = (i // 8) * 4
-        j = i % 8
-        c = pl.ds(pl.multiple_of(j * 256, 256), 256)
+        s = (i // 4) * 4
+        j = i % 4
+        c = pl.ds(pl.multiple_of(j * COLS, COLS), COLS)
         a = u_buf[pl.ds(s, 4)].reshape(4 * HALF, D)
-        kv[pl.ds(2 * OWN + s, 4), :, c] = dot_nt(a, w_buf[c, :]).astype(BF16).reshape(4, HALF, 256)
+        kv[pl.ds(2 * OWN + s, 4), :, c] = dot_nt(a, w_buf[c, :]).astype(BF16).reshape(4, HALF, COLS)
         return carry
 
-    lax.fori_loop(0, 16, fill, 0)
+    lax.fori_loop(0, 8, fill, 0)
     c4.wait()
     c5.wait()
     c6.wait()

time: 1360 us -> 1290 us (0.949)
  Pallas kernels: 825 us -> 729 us
  waiting for transfers between devices: 249 us -> 281 us
    pallas_call x18, Pallas kernels: 185 us -> 137 us  [project_call(): pl.pallas_call(project_kernel, grid=(cols // blk,), out_shape=jax.ShapeDt...]
    pallas_call x20, Pallas kernels: 450 us -> 414 us  [dense_call(): pl.pallas_call(functools.partial(dense_kernel, do_c=do_c, do_a=do_a, ns=n...]
    ppermute x84, waiting for transfers between devices: 232 us -> 264 us  [move(): out.append(lax.ppermute(vals[p], axes, pairs))]
  transfers between devices with their start and end apart: 93 -> 93, of which waited for: 38 -> 43; matrix products, arithmetic and copies ran while one was open for 1% -> 1% of each run, Pallas kernels for 29% -> 26%
where the time goes in v3:
time: 1290 us; the launch traced here: 1280 us
  Pallas kernels  729 us (57%)
  waiting for transfers between devices  281 us (22%)
  starting transfers between devices  169 us (13%)
  blocking collectives  53.5 us (4%)
  local copies, waits for them, and re-layouts  36.7 us (3%)
    pallas_call x20, Pallas kernels, dense_call(): pl.pallas_call(functools.partial(dense_kernel, do_c=do_c, do_a=do_a, ns=n...  414 us
    ppermute x84, waiting for transfers between devices, move(): out.append(lax.ppermute(vals[p], axes, pairs))  264 us
    pallas_call x6, Pallas kernels, halo_call(): pl.pallas_call(functools.partial(halo_kernel, layer=layer), out_shape=[ja...  166 us
    ppermute x84, starting transfers between devices, move(): out.append(lax.ppermute(vals[p], axes, pairs))  161 us
    pallas_call x18, Pallas kernels, project_call(): pl.pallas_call(project_kernel, grid=(cols // blk,), out_shape=jax.ShapeDt...  137 us
    all_gather x1, blocking collectives, body(): lax.all_gather(small, group, axis=0).reshape(nz, 4, 17 + n_steps, 256)  32.3 us
  transfers between devices with their start and end apart: 93, of which 43 were waited for; matrix products, arithmetic and copies ran while one was open for 1% of the time, Pallas kernels for 26%

profile of v3, /device:TPU:0, one launch (start us, length us, event | category | flops | bytes accessed | tf_op | source)
XLA Modules:
  0.0 1281.3 jit_solution(9064698892700119946)
XLA Ops:
  8.2 32.3 %all-gather.2 = f32[16,19,256]{2,1,0:T(8,128)S(1)} all-gather(f32[1,19,256]{2,1,0:T(8,128)S(1)} %maximum_bitcast_fusion.1), channel_id=2, replica_groups=mesh['videos'=2,'tokens'=4,'frames'=4] {'tokens','frames'}, dimensions={0}, use_global_device_ids=true | all-gather | bytes 330752 | tf_op jit(solution)/shard_map/all_gather | solution.py:404
  73.3 16.7 %dense.21 = (f32[512,1024]{1,0:T(8,128)}, bf16[2,128,1024]{2,1,0:T(8,128)(2,1)}, bf16[2,128,1024]{2,1,0:T(8,128)(2,1)}) custom-call(f32[512,1024]{1,0:T(8,128)} %get-tuple-element.109.refs_0_, f32[2,6,1024]{2,1,0:T(8,128)} %get-tuple-element.114.refs_1_.refs_3_, bf16[3,3072,1024]{2,1,0:T(8,128)(2,1)} %bitcast.88, bf16[3,1024,1024]{2,1,0:T(8,128)(2,1)} %bitcast.112), custom_call_target="tpu_custom_call" | custom-call | flops 4294967296 | bytes 4194304 | tf_op jit(solution)/shard_map/dense/pallas_call | solution.py:217
  190.7 27.7 %temporal_halo.6 = (bf16[4,128,1024]{2,1,0:T(8,128)(2,1)}, bf16[4,128,1024]{2,1,0:T(8,128)(2,1)}) custom-call(bf16[8,128,1024]{2,1,0:T(8,128)(2,1)} %project.18.refs_0_, bf16[8,128,2048]{2,1,0:T(8,128)(2,1)} %project.19.refs_1_, bf16[8,128,2048]{2,1,0:T(8,128)(2,1)} %project.20.refs_2_, bf16[2,128,1024]{2,1,0:T(8,128)(2,1)} %collective-permute-done.6.refs_3_, ...), custom_call_target="tpu_custom_call" | custom-call | flops 8589934592 | bytes 16777216 | tf_op jit(solution)/shard_map/temporal_halo/pallas_call | solution.py:333
  221.4 31.2 %dense.22 = (f32[512,1024]{1,0:T(8,128)}, bf16[2,128,1024]{2,1,0:T(8,128)(2,1)}, bf16[2,128,1024]{2,1,0:T(8,128)(2,1)}) custom-call(f32[512,1024]{1,0:T(8,128)} %get-tuple-element.50.refs_0_, bf16[4,128,1024]{2,1,0:T(8,128)(2,1)} %get-tuple-element.55.refs_1_, bf16[4,128,1024]{2,1,0:T(8,128)(2,1)} %collective-permute-done.14.refs_2_, ...), custom_call_target="tpu_custom_call" | custom-call | flops 13958643712 | bytes 4194304 | tf_op jit(solution)/shard_map/dense/pallas_call | solution.py:217
  260.5 19.5 %dense.23.refs_0_ = f32[512,1024]{1,0:T(8,128)} custom-call(f32[512,1024]{1,0:T(8,128)} %get-tuple-element.59.refs_0_, bf16[4,128,1024]{2,1,0:T(8,128)(2,1)} %get-tuple-element.55.refs_1_, bf16[4,128,1024]{2,1,0:T(8,128)(2,1)} %collective-permute-done.14.refs_2_, f32[2,6,1024]{2,1,0:T(8,128)} %get-tuple-element.114.refs_1_.refs_3_, ...), custom_call_target="tpu_custom_call" | custom-call | flops 9663676416 | bytes 4194304 | tf_op jit(solution)/shard_map/dense/pallas_call | solution.py:217
  280.0 16.6 %dense.24 = (f32[512,1024]{1,0:T(8,128)}, bf16[2,128,1024]{2,1,0:T(8,128)(2,1)}, bf16[2,128,1024]{2,1,0:T(8,128)(2,1)}) custom-call(f32[512,1024]{1,0:T(8,128)} %dense.23.refs_0_, f32[2,6,1024]{2,1,0:T(8,128)} %get-tuple-element.112.refs_1_.refs_3_, bf16[3,3072,1024]{2,1,0:T(8,128)(2,1)} %bitcast.90, bf16[3,1024,1024]{2,1,0:T(8,128)(2,1)} %bitcast.114), custom_call_target="tpu_custom_call" | custom-call | flops 4294967296 | bytes 4194304 | tf_op jit(solution)/shard_map/dense/pallas_call | solution.py:217
  383.2 27.7 %temporal_halo.7 = (bf16[4,128,1024]{2,1,0:T(8,128)(2,1)}, bf16[4,128,1024]{2,1,0:T(8,128)(2,1)}) custom-call(bf16[8,128,1024]{2,1,0:T(8,128)(2,1)} %project.21.refs_0_, bf16[8,128,2048]{2,1,0:T(8,128)(2,1)} %project.22.refs_1_, bf16[8,128,2048]{2,1,0:T(8,128)(2,1)} %project.23.refs_2_, bf16[2,128,1024]{2,1,0:T(8,128)(2,1)} %collective-permute-done.21.refs_3_, ...), custom_call_target="tpu_custom_call" | custom-call | flops 8589934592 | bytes 16777216 | tf_op jit(solution)/shard_map/temporal_halo/pallas_call | solution.py:333
  414.0 31.2 %dense.25 = (f32[512,1024]{1,0:T(8,128)}, bf16[2,128,1024]{2,1,0:T(8,128)(2,1)}, bf16[2,128,1024]{2,1,0:T(8,128)(2,1)}) custom-call(f32[512,1024]{1,0:T(8,128)} %get-tuple-element.57.refs_0_, bf16[4,128,1024]{2,1,0:T(8,128)(2,1)} %get-tuple-element.63.refs_1_, bf16[4,128,1024]{2,1,0:T(8,128)(2,1)} %collective-permute-done.29.refs_2_, ...), custom_call_target="tpu_custom_call" | custom-call | flops 13958643712 | bytes 4194304 | tf_op jit(solution)/shard_map/dense/pallas_call | solution.py:217
  452.5 19.5 %dense.26.refs_0_ = f32[512,1024]{1,0:T(8,128)} custom-call(f32[512,1024]{1,0:T(8,128)} %get-tuple-element.67.refs_0_, bf16[4,128,1024]{2,1,0:T(8,128)(2,1)} %get-tuple-element.63.refs_1_, bf16[4,128,1024]{2,1,0:T(8,128)(2,1)} %collective-permute-done.29.refs_2_, f32[2,6,1024]{2,1,0:T(8,128)} %get-tuple-element.112.refs_1_.refs_3_, ...), custom_call_target="tpu_custom_call" | custom-call | flops 9663676416 | bytes 4194304 | tf_op jit(solution)/shard_map/dense/pallas_call | solution.py:217
  574.3 27.7 %temporal_halo.8 = (bf16[4,128,1024]{2,1,0:T(8,128)(2,1)}, bf16[4,128,1024]{2,1,0:T(8,128)(2,1)}) custom-call(bf16[8,128,1024]{2,1,0:T(8,128)(2,1)} %project.24.refs_0_, bf16[8,128,2048]{2,1,0:T(8,128)(2,1)} %project.25.refs_1_, bf16[8,128,2048]{2,1,0:T(8,128)(2,1)} %project.26.refs_2_, bf16[2,128,1024]{2,1,0:T(8,128)(2,1)} %collective-permute-done.36.refs_3_, ...), custom_call_target="tpu_custom_call" | custom-call | flops 8589934592 | bytes 16777216 | tf_op jit(solution)/shard_map/temporal_halo/pallas_call | solution.py:333
  605.0 19.5 %dense.29 = f32[512,1024]{1,0:T(8,128)} custom-call(f32[512,1024]{1,0:T(8,128)} %get-tuple-element.73.refs_0_, bf16[4,128,1024]{2,1,0:T(8,128)(2,1)} %get-tuple-element.71.refs_1_, bf16[4,128,1024]{2,1,0:T(8,128)(2,1)} %collective-permute-done.44.refs_2_, f32[2,6,1024]{2,1,0:T(8,128)} %get-tuple-element.111.refs_1_.refs_3_, ...), custom_call_target="tpu_custom_call" | custom-call | flops 9663676416 | bytes 4194304 | tf_op jit(solution)/shard_map/dense/pallas_call | solution.py:217
  624.5 19.4 %dense.28 = f32[512,1024]{1,0:T(8,128)} custom-call(f32[512,1024]{1,0:T(8,128)} %get-tuple-element.65.refs_0_, bf16[4,128,1024]{2,1,0:T(8,128)(2,1)} %get-tuple-element.71.refs_1_, bf16[4,128,1024]{2,1,0:T(8,128)(2,1)} %collective-permute-done.44.refs_2_, f32[2,6,1024]{2,1,0:T(8,128)} %get-tuple-element.110.refs_7_.refs_3_, ...), custom_call_target="tpu_custom_call" | custom-call | flops 9663676416 | bytes 4194304 | tf_op jit(solution)/shard_map/dense/pallas_call | solution.py:217
  681.5 16.6 %dense.31 = (f32[512,1024]{1,0:T(8,128)}, bf16[2,128,1024]{2,1,0:T(8,128)(2,1)}, bf16[2,128,1024]{2,1,0:T(8,128)(2,1)}) custom-call(f32[512,1024]{1,0:T(8,128)} %get-tuple-element.107.refs_0_, f32[2,6,1024]{2,1,0:T(8,128)} %get-tuple-element.114.refs_1_.refs_3_, bf16[3,3072,1024]{2,1,0:T(8,128)(2,1)} %bitcast.94, bf16[3,1024,1024]{2,1,0:T(8,128)(2,1)} %bitcast.118), custom_call_target="tpu_custom_call" | custom-call | flops 4294967296 | bytes 4194304 | tf_op jit(solution)/shard_map/dense/pallas_call | solution.py:217
  786.0 27.7 %temporal_halo.9 = (bf16[4,128,1024]{2,1,0:T(8,128)(2,1)}, bf16[4,128,1024]{2,1,0:T(8,128)(2,1)}) custom-call(bf16[8,128,1024]{2,1,0:T(8,128)(2,1)} %project.27.refs_0_, bf16[8,128,2048]{2,1,0:T(8,128)(2,1)} %project.28.refs_1_, bf16[8,128,2048]{2,1,0:T(8,128)(2,1)} %project.29.refs_2_, bf16[2,128,1024]{2,1,0:T(8,128)(2,1)} %collective-permute-done.52.refs_3_, ...), custom_call_target="tpu_custom_call" | custom-call | flops 8589934592 | bytes 16777216 | tf_op jit(solution)/shard_map/temporal_halo/pallas_call | solution.py:333
  816.7 31.3 %dense.32 = (f32[512,1024]{1,0:T(8,128)}, bf16[2,128,1024]{2,1,0:T(8,128)(2,1)}, bf16[2,128,1024]{2,1,0:T(8,128)(2,1)}) custom-call(f32[512,1024]{1,0:T(8,128)} %get-tuple-element.74.refs_0_, bf16[4,128,1024]{2,1,0:T(8,128)(2,1)} %get-tuple-element.79.refs_1_, bf16[4,128,1024]{2,1,0:T(8,128)(2,1)} %collective-permute-done.60.refs_2_, ...), custom_call_target="tpu_custom_call" | custom-call | flops 13958643712 | bytes 4194304 | tf_op jit(solution)/shard_map/dense/pallas_call | solution.py:217
  855.6 19.5 %dense.33.refs_0_ = f32[512,1024]{1,0:T(8,128)} custom-call(f32[512,1024]{1,0:T(8,128)} %get-tuple-element.83.refs_0_, bf16[4,128,1024]{2,1,0:T(8,128)(2,1)} %get-tuple-element.79.refs_1_, bf16[4,128,1024]{2,1,0:T(8,128)(2,1)} %collective-permute-done.60.refs_2_, f32[2,6,1024]{2,1,0:T(8,128)} %get-tuple-element.114.refs_1_.refs_3_, ...), custom_call_target="tpu_custom_call" | custom-call | flops 9663676416 | bytes 4194304 | tf_op jit(solution)/shard_map/dense/pallas_call | solution.py:217
  875.1 16.6 %dense.34 = (f32[512,1024]{1,0:T(8,128)}, bf16[2,128,1024]{2,1,0:T(8,128)(2,1)}, bf16[2,128,1024]{2,1,0:T(8,128)(2,1)}) custom-call(f32[512,1024]{1,0:T(8,128)} %dense.33.refs_0_, f32[2,6,1024]{2,1,0:T(8,128)} %get-tuple-element.112.refs_1_.refs_3_, bf16[3,3072,1024]{2,1,0:T(8,128)(2,1)} %bitcast.96, bf16[3,1024,1024]{2,1,0:T(8,128)(2,1)} %bitcast.120), custom_call_target="tpu_custom_call" | custom-call | flops 4294967296 | bytes 4194304 | tf_op jit(solution)/shard_map/dense/pallas_call | solution.py:217
  977.3 27.7 %temporal_halo.10 = (bf16[4,128,1024]{2,1,0:T(8,128)(2,1)}, bf16[4,128,1024]{2,1,0:T(8,128)(2,1)}) custom-call(bf16[8,128,1024]{2,1,0:T(8,128)(2,1)} %project.30.refs_0_, bf16[8,128,2048]{2,1,0:T(8,128)(2,1)} %project.31.refs_1_, bf16[8,128,2048]{2,1,0:T(8,128)(2,1)} %project.32.refs_2_, bf16[2,128,1024]{2,1,0:T(8,128)(2,1)} %collective-permute-done.67.refs_3_, ...), custom_call_target="tpu_custom_call" | custom-call | flops 8589934592 | bytes 16777216 | tf_op jit(solution)/shard_map/temporal_halo/pallas_call | solution.py:333
  1008.1 31.3 %dense.35 = (f32[512,1024]{1,0:T(8,128)}, bf16[2,128,1024]{2,1,0:T(8,128)(2,1)}, bf16[2,128,1024]{2,1,0:T(8,128)(2,1)}) custom-call(f32[512,1024]{1,0:T(8,128)} %get-tuple-element.81.refs_0_, bf16[4,128,1024]{2,1,0:T(8,128)(2,1)} %get-tuple-element.87.refs_1_, bf16[4,128,1024]{2,1,0:T(8,128)(2,1)} %collective-permute-done.75.refs_2_, ...), custom_call_target="tpu_custom_call" | custom-call | flops 13958643712 | bytes 4194304 | tf_op jit(solution)/shard_map/dense/pallas_call | solution.py:217
  1046.7 19.5 %dense.36.refs_0_ = f32[512,1024]{1,0:T(8,128)} custom-call(f32[512,1024]{1,0:T(8,128)} %get-tuple-element.91.refs_0_, bf16[4,128,1024]{2,1,0:T(8,128)(2,1)} %get-tuple-element.87.refs_1_, bf16[4,128,1024]{2,1,0:T(8,128)(2,1)} %collective-permute-done.75.refs_2_, f32[2,6,1024]{2,1,0:T(8,128)} %get-tuple-element.112.refs_1_.refs_3_, ...), custom_call_target="tpu_custom_call" | custom-call | flops 9663676416 | bytes 4194304 | tf_op jit(solution)/shard_map/dense/pallas_call | solution.py:217
  1168.5 27.6 %temporal_halo.11 = (bf16[4,128,1024]{2,1,0:T(8,128)(2,1)}, bf16[4,128,1024]{2,1,0:T(8,128)(2,1)}) custom-call(bf16[8,128,1024]{2,1,0:T(8,128)(2,1)} %project.33.refs_0_, bf16[8,128,2048]{2,1,0:T(8,128)(2,1)} %project.34.refs_1_, bf16[8,128,2048]{2,1,0:T(8,128)(2,1)} %project.35.refs_2_, bf16[2,128,1024]{2,1,0:T(8,128)(2,1)} %collective-permute-done.82.refs_3_, ...), custom_call_target="tpu_custom_call" | custom-call | flops 8589934592 | bytes 16777216 | tf_op jit(solution)/shard_map/temporal_halo/pallas_call | solution.py:333
  1199.2 19.4 %dense.39 = f32[512,1024]{1,0:T(8,128)} custom-call(f32[512,1024]{1,0:T(8,128)} %get-tuple-element.97.refs_0_, bf16[4,128,1024]{2,1,0:T(8,128)(2,1)} %get-tuple-element.95.refs_1_, bf16[4,128,1024]{2,1,0:T(8,128)(2,1)} %collective-permute-done.90.refs_2_, f32[2,6,1024]{2,1,0:T(8,128)} %get-tuple-element.111.refs_1_.refs_3_, ...), custom_call_target="tpu_custom_call" | custom-call | flops 9663676416 | bytes 4194304 | tf_op jit(solution)/shard_map/dense/pallas_call | solution.py:217
  1218.6 19.4 %dense.38 = f32[512,1024]{1,0:T(8,128)} custom-call(f32[512,1024]{1,0:T(8,128)} %get-tuple-element.89.refs_0_, bf16[4,128,1024]{2,1,0:T(8,128)(2,1)} %get-tuple-element.95.refs_1_, bf16[4,128,1024]{2,1,0:T(8,128)(2,1)} %collective-permute-done.90.refs_2_, f32[2,6,1024]{2,1,0:T(8,128)} %get-tuple-element.110.refs_7_.refs_3_, ...), custom_call_target="tpu_custom_call" | custom-call | flops 9663676416 | bytes 4194304 | tf_op jit(solution)/shard_map/dense/pallas_call | solution.py:217
  1246.4 21.3 %all-gather.3 = f32[16,6,1024]{2,1,0:T(8,128)S(1)} all-gather(f32[1,6,1024]{2,1,0:T(8,128)S(1)} %maximum_bitcast_fusion), channel_id=3, replica_groups=mesh['videos'=2,'tokens'=4,'frames'=4] {'tokens','frames'}, dimensions={0}, use_global_device_ids=true | all-gather | bytes 417792 | tf_op jit(solution)/shard_map/all_gather | solution.py:466
  (342 shorter events, 712.4 us)
Async XLA Ops:
  3.5 46.9 %all-to-all-start = ((f32[4,4,3,6,1024]{4,1,3,2,0:T(4,128)}), f32[4,4,3,6,1024]{4,1,3,2,0:T(4,128)}, u32[]{:S(2)}, u32[]{:S(2)}) async-start(f32[4,4,3,6,1024]{4,1,3,2,0:T(4,128)} %copy.78), calls=%async_computation | async-start | bytes 2359296 | tf_op jit(solution)/shard_map/all_to_all | solution.py:409
  94.3 43.6 %collective-permute-start.8 = (bf16[2,128,1024]{2,1,0:T(8,128)(2,1)}, bf16[2,128,1024]{2,1,0:T(8,128)(2,1)}, u32[]{:S(2)}, u32[]{:S(2)}) collective-permute-start(bf16[2,128,1024]{2,1,0:T(8,128)(2,1)} %get-tuple-element.53), channel_id=1, source_target_pairs={{0,3},{1,2},{4,7},{5,6},{8,11},{9,10},{12,15},{13,14},{16,19},{17,... | collective-permute-start | bytes 1572872 | tf_op jit(solution)/shard_map/ppermute | solution.py:436
  98.4 42.4 %collective-permute-start = (bf16[2,128,1024]{2,1,0:T(8,128)(2,1)}, bf16[2,128,1024]{2,1,0:T(8,128)(2,1)}, u32[]{:S(2)}, u32[]{:S(2)}) collective-permute-start(bf16[2,128,1024]{2,1,0:T(8,128)(2,1)} %get-tuple-element.53), channel_id=1, source_target_pairs={{0,1},{1,0},{2,3},{3,2},{4,5},{5,4},{6,7},{7,6},{8,9},{9,8},{10,11... | collective-permute-start | bytes 1572872 | tf_op jit(solution)/shard_map/ppermute | solution.py:436
  98.6 43.5 %collective-permute-start.6 = (bf16[2,128,1024]{2,1,0:T(8,128)(2,1)S(1)}, bf16[2,128,1024]{2,1,0:T(8,128)(2,1)}, u32[]{:S(2)}, u32[]{:S(2)}) collective-permute-start(bf16[2,128,1024]{2,1,0:T(8,128)(2,1)S(1)} %copy-done.14), channel_id=1, source_target_pairs={{0,2},{1,3},{4,6},{5,7},{8,10},{9,11},{12,14},{13,15},{16,18},{17,... | collective-permute-start | bytes 1572872 | tf_op jit(solution)/shard_map/ppermute | solution.py:436
  105.3 38.1 %collective-permute-start.9 = (bf16[2,128,1024]{2,1,0:T(8,128)(2,1)}, bf16[2,128,1024]{2,1,0:T(8,128)(2,1)}, u32[]{:S(2)}, u32[]{:S(2)}) collective-permute-start(bf16[2,128,1024]{2,1,0:T(8,128)(2,1)} %get-tuple-element.54), channel_id=1, source_target_pairs={{0,3},{1,2},{4,7},{5,6},{8,11},{9,10},{12,15},{13,14},{16,19},{17,... | collective-permute-start | bytes 1572872 | tf_op jit(solution)/shard_map/ppermute | solution.py:436
  143.4 36.9 %collective-permute-start.13 = (bf16[2,128,1024]{2,1,0:T(8,128)(2,1)}, bf16[2,128,1024]{2,1,0:T(8,128)(2,1)}, u32[]{:S(2)}, u32[]{:S(2)}) collective-permute-start(bf16[2,128,1024]{2,1,0:T(8,128)(2,1)} %collective-permute-done.5.refs_3_), channel_id=1, source_target_pairs={{2,0},{3,1},{6,4},{7,5},{10,8},{11,9},{14,12},{15,13},{18,16},{19,... | collective-permute-start | bytes 1572872 | tf_op jit(solution)/shard_map/ppermute | solution.py:436
  144.7 46.0 %collective-permute-start.11 = (bf16[2,128,1024]{2,1,0:T(8,128)(2,1)}, bf16[2,128,1024]{2,1,0:T(8,128)(2,1)}, u32[]{:S(2)}, u32[]{:S(2)}) collective-permute-start(bf16[2,128,1024]{2,1,0:T(8,128)(2,1)} %collective-permute-done.3.refs_1_), channel_id=1, source_target_pairs={{2,0},{3,1},{6,4},{7,5},{10,8},{11,9},{14,12},{15,13},{18,16},{19,... | collective-permute-start | bytes 1572872 | tf_op jit(solution)/shard_map/ppermute | solution.py:436
  252.7 51.2 %collective-permute-start.19 = (bf16[2,128,1024]{2,1,0:T(8,128)(2,1)}, bf16[2,128,1024]{2,1,0:T(8,128)(2,1)}, u32[]{:S(2)}, u32[]{:S(2)}) collective-permute-start(bf16[2,128,1024]{2,1,0:T(8,128)(2,1)} %get-tuple-element.61), channel_id=1, source_target_pairs={{0,5},{1,4},{2,7},{3,6},{4,9},{5,8},{6,11},{7,10},{8,13},{9,12},{1... | collective-permute-start | bytes 1572872 | tf_op jit(solution)/shard_map/ppermute | solution.py:436
  257.6 46.5 %collective-permute-start.17 = (bf16[2,128,1024]{2,1,0:T(8,128)(2,1)}, bf16[2,128,1024]{2,1,0:T(8,128)(2,1)}, u32[]{:S(2)}, u32[]{:S(2)}) collective-permute-start(bf16[2,128,1024]{2,1,0:T(8,128)(2,1)} %get-tuple-element.58.refs_0_), channel_id=1, source_target_pairs={{0,4},{1,5},{2,6},{3,7},{4,8},{5,9},{6,10},{7,11},{8,12},{9,13},{1... | collective-permute-start | bytes 1572872 | tf_op jit(solution)/shard_map/ppermute | solution.py:436
  338.1 34.5 %collective-permute-start.28 = (bf16[2,128,1024]{2,1,0:T(8,128)(2,1)}, bf16[2,128,1024]{2,1,0:T(8,128)(2,1)}, u32[]{:S(2)}, u32[]{:S(2)}) collective-permute-start(bf16[2,128,1024]{2,1,0:T(8,128)(2,1)} %collective-permute-done.20.refs_3_), channel_id=1, source_target_pairs={{2,0},{3,1},{6,4},{7,5},{10,8},{11,9},{14,12},{15,13},{18,16},{19,... | collective-permute-start | bytes 1572872 | tf_op jit(solution)/shard_map/ppermute | solution.py:436
  339.4 43.8 %collective-permute-start.26 = (bf16[2,128,1024]{2,1,0:T(8,128)(2,1)}, bf16[2,128,1024]{2,1,0:T(8,128)(2,1)}, u32[]{:S(2)}, u32[]{:S(2)}) collective-permute-start(bf16[2,128,1024]{2,1,0:T(8,128)(2,1)} %collective-permute-done.18.refs_1_), channel_id=1, source_target_pairs={{2,0},{3,1},{6,4},{7,5},{10,8},{11,9},{14,12},{15,13},{18,16},{19,... | collective-permute-start | bytes 1572872 | tf_op jit(solution)/shard_map/ppermute | solution.py:436
  445.2 49.8 %collective-permute-start.34 = (bf16[2,128,1024]{2,1,0:T(8,128)(2,1)}, bf16[2,128,1024]{2,1,0:T(8,128)(2,1)}, u32[]{:S(2)}, u32[]{:S(2)}) collective-permute-start(bf16[2,128,1024]{2,1,0:T(8,128)(2,1)} %get-tuple-element.69), channel_id=1, source_target_pairs={{0,5},{1,4},{2,7},{3,6},{4,9},{5,8},{6,11},{7,10},{8,13},{9,12},{1... | collective-permute-start | bytes 1572872 | tf_op jit(solution)/shard_map/ppermute | solution.py:436
  450.1 45.1 %collective-permute-start.32 = (bf16[2,128,1024]{2,1,0:T(8,128)(2,1)}, bf16[2,128,1024]{2,1,0:T(8,128)(2,1)}, u32[]{:S(2)}, u32[]{:S(2)}) collective-permute-start(bf16[2,128,1024]{2,1,0:T(8,128)(2,1)} %get-tuple-element.66.refs_0_), channel_id=1, source_target_pairs={{0,4},{1,5},{2,6},{3,7},{4,8},{5,9},{6,10},{7,11},{8,12},{9,13},{1... | collective-permute-start | bytes 1572872 | tf_op jit(solution)/shard_map/ppermute | solution.py:436
  529.2 34.5 %collective-permute-start.43 = (bf16[2,128,1024]{2,1,0:T(8,128)(2,1)}, bf16[2,128,1024]{2,1,0:T(8,128)(2,1)}, u32[]{:S(2)}, u32[]{:S(2)}) collective-permute-start(bf16[2,128,1024]{2,1,0:T(8,128)(2,1)} %collective-permute-done.35.refs_3_), channel_id=1, source_target_pairs={{2,0},{3,1},{6,4},{7,5},{10,8},{11,9},{14,12},{15,13},{18,16},{19,... | collective-permute-start | bytes 1572872 | tf_op jit(solution)/shard_map/ppermute | solution.py:436
  530.5 43.8 %collective-permute-start.41 = (bf16[2,128,1024]{2,1,0:T(8,128)(2,1)}, bf16[2,128,1024]{2,1,0:T(8,128)(2,1)}, u32[]{:S(2)}, u32[]{:S(2)}) collective-permute-start(bf16[2,128,1024]{2,1,0:T(8,128)(2,1)} %collective-permute-done.33.refs_1_), channel_id=1, source_target_pairs={{2,0},{3,1},{6,4},{7,5},{10,8},{11,9},{14,12},{15,13},{18,16},{19,... | collective-permute-start | bytes 1572872 | tf_op jit(solution)/shard_map/ppermute | solution.py:436
  739.4 36.1 %collective-permute-start.59 = (bf16[2,128,1024]{2,1,0:T(8,128)(2,1)}, bf16[2,128,1024]{2,1,0:T(8,128)(2,1)}, u32[]{:S(2)}, u32[]{:S(2)}) collective-permute-start(bf16[2,128,1024]{2,1,0:T(8,128)(2,1)} %collective-permute-done.51.refs_3_), channel_id=1, source_target_pairs={{2,0},{3,1},{6,4},{7,5},{10,8},{11,9},{14,12},{15,13},{18,16},{19,... | collective-permute-start | bytes 1572872 | tf_op jit(solution)/shard_map/ppermute | solution.py:436
  740.7 45.3 %collective-permute-start.57 = (bf16[2,128,1024]{2,1,0:T(8,128)(2,1)}, bf16[2,128,1024]{2,1,0:T(8,128)(2,1)}, u32[]{:S(2)}, u32[]{:S(2)}) collective-permute-start(bf16[2,128,1024]{2,1,0:T(8,128)(2,1)} %collective-permute-done.49.refs_1_), channel_id=1, source_target_pairs={{2,0},{3,1},{6,4},{7,5},{10,8},{11,9},{14,12},{15,13},{18,16},{19,... | collective-permute-start | bytes 1572872 | tf_op jit(solution)/shard_map/ppermute | solution.py:436
  848.0 50.1 %collective-permute-start.65 = (bf16[2,128,1024]{2,1,0:T(8,128)(2,1)}, bf16[2,128,1024]{2,1,0:T(8,128)(2,1)}, u32[]{:S(2)}, u32[]{:S(2)}) collective-permute-start(bf16[2,128,1024]{2,1,0:T(8,128)(2,1)} %get-tuple-element.85), channel_id=1, source_target_pairs={{0,5},{1,4},{2,7},{3,6},{4,9},{5,8},{6,11},{7,10},{8,13},{9,12},{1... | collective-permute-start | bytes 1572872 | tf_op jit(solution)/shard_map/ppermute | solution.py:436
  852.9 45.4 %collective-permute-start.63 = (bf16[2,128,1024]{2,1,0:T(8,128)(2,1)}, bf16[2,128,1024]{2,1,0:T(8,128)(2,1)}, u32[]{:S(2)}, u32[]{:S(2)}) collective-permute-start(bf16[2,128,1024]{2,1,0:T(8,128)(2,1)} %get-tuple-element.82.refs_0_), channel_id=1, source_target_pairs={{0,4},{1,5},{2,6},{3,7},{4,8},{5,9},{6,10},{7,11},{8,12},{9,13},{1... | collective-permute-start | bytes 1572872 | tf_op jit(solution)/shard_map/ppermute | solution.py:436
  933.6 43.8 %collective-permute-start.72 = (bf16[2,128,1024]{2,1,0:T(8,128)(2,1)}, bf16[2,128,1024]{2,1,0:T(8,128)(2,1)}, u32[]{:S(2)}, u32[]{:S(2)}) collective-permute-start(bf16[2,128,1024]{2,1,0:T(8,128)(2,1)} %collective-permute-done.64.refs_1_), channel_id=1, source_target_pairs={{2,0},{3,1},{6,4},{7,5},{10,8},{11,9},{14,12},{15,13},{18,16},{19,... | collective-permute-start | bytes 1572872 | tf_op jit(solution)/shard_map/ppermute | solution.py:436
  1039.4 49.8 %collective-permute-start.80 = (bf16[2,128,1024]{2,1,0:T(8,128)(2,1)}, bf16[2,128,1024]{2,1,0:T(8,128)(2,1)}, u32[]{:S(2)}, u32[]{:S(2)}) collective-permute-start(bf16[2,128,1024]{2,1,0:T(8,128)(2,1)} %get-tuple-element.93), channel_id=1, source_target_pairs={{0,5},{1,4},{2,7},{3,6},{4,9},{5,8},{6,11},{7,10},{8,13},{9,12},{1... | collective-permute-start | bytes 1572872 | tf_op jit(solution)/shard_map/ppermute | solution.py:436
  1044.3 45.1 %collective-permute-start.78 = (bf16[2,128,1024]{2,1,0:T(8,128)(2,1)}, bf16[2,128,1024]{2,1,0:T(8,128)(2,1)}, u32[]{:S(2)}, u32[]{:S(2)}) collective-permute-start(bf16[2,128,1024]{2,1,0:T(8,128)(2,1)} %get-tuple-element.90.refs_0_), channel_id=1, source_target_pairs={{0,4},{1,5},{2,6},{3,7},{4,8},{5,9},{6,10},{7,11},{8,12},{9,13},{1... | collective-permute-start | bytes 1572872 | tf_op jit(solution)/shard_map/ppermute | solution.py:436
  1123.4 34.4 %collective-permute-start.89 = (bf16[2,128,1024]{2,1,0:T(8,128)(2,1)}, bf16[2,128,1024]{2,1,0:T(8,128)(2,1)}, u32[]{:S(2)}, u32[]{:S(2)}) collective-permute-start(bf16[2,128,1024]{2,1,0:T(8,128)(2,1)} %collective-permute-done.81.refs_3_), channel_id=1, source_target_pairs={{2,0},{3,1},{6,4},{7,5},{10,8},{11,9},{14,12},{15,13},{18,16},{19,... | collective-permute-start | bytes 1572872 | tf_op jit(solution)/shard_map/ppermute | solution.py:436
  1124.7 43.8 %collective-permute-start.87 = (bf16[2,128,1024]{2,1,0:T(8,128)(2,1)}, bf16[2,128,1024]{2,1,0:T(8,128)(2,1)}, u32[]{:S(2)}, u32[]{:S(2)}) collective-permute-start(bf16[2,128,1024]{2,1,0:T(8,128)(2,1)} %collective-permute-done.79.refs_1_), channel_id=1, source_target_pairs={{2,0},{3,1},{6,4},{7,5},{10,8},{11,9},{14,12},{15,13},{18,16},{19,... | collective-permute-start | bytes 1572872 | tf_op jit(solution)/shard_map/ppermute | solution.py:436
  (100 other events, 2016.4 us)
